TPU v7x, 32 devices: a whole 2x2x4 slice. The times are simulated.
32 devices in a mesh: grp: 4 (over y, x), dev: 8 (over z, core).
Axes of the slice: x: 2, y: 2, z: 4, core: 2. Of those that a mesh axis runs over, the one named last changes fastest.
Arguments:
- table: float32 [262144, 128], P(('grp', 'dev')), may hold values from -6 to 6
- cold_grads: float32 [131072, 128], P(('grp', 'dev')), may hold values from -6 to 6
- cold_owner: int32 [131072, 1], P(('grp', 'dev')), may hold values from 0 to 31; in each aligned block of 4096 rows (0 to 4095, 4096 to 8191, ...) at most 256 rows name the same one
- cold_row: int32 [131072], P(('grp', 'dev')), may hold values from 0 to 8191
- hot_grads: float32 [32768, 128], P(('grp', 'dev')), may hold values from -6 to 6
- hot_slot: int32 [32768], P(('grp', 'dev')), may hold values from 0 to 255
- hot_ids: int32 [256], replicated, may hold values from 0 to 262143, as said below
Outputs:
- new_table: float32 [262144, 128], P(('grp', 'dev'))
Inputs may be any that keep to these rules, and one draw needn't show every extreme that they name: `cold_owner`: among the 4096 rare-row lookups of one device no owner is named more than 256 times, a bound that some block reaches. `hot_ids`: all entries differ.
All inputs are finite; a program needn't handle non-finite values.
Results may differ from a plain program's by a relative error of at most 0.00005.
Values sent between devices are 32-bit elements; how exact they have to be, the bound alone decides.
No kernel may reach another device: no remote copies, remote signals or barrier semaphores. Data moves between devices by JAX's collectives and lax.ppermute only.
A program may use at most 64 MiB of HBM per device.

v0:
```python
import functools

import jax
import jax.numpy as jnp
from jax import lax
from jax.experimental import pallas as pl
from jax.experimental.pallas import tpu as pltpu
from jax.sharding import PartitionSpec as P


LEARN = 0.05
LANES = 128
UNROLL = 32
WAYS = 4
AXES = ("grp", "dev")
MIB = 1024 * 1024
ANY = pl.BlockSpec(memory_space=pl.ANY)
VMEM = pl.BlockSpec(memory_space=pltpu.VMEM)
HBM = pl.BlockSpec(memory_space=pltpu.HBM)
SMEM = pl.BlockSpec(memory_space=pltpu.SMEM)


def in_hbm(x):
    return pltpu.with_memory_space_constraint(x, pltpu.HBM)


def id_rows_of(slots):
    return -(-slots // LANES)


def plan_kernel(n, n_dev, slots, rows_dev, ks, owner_ref, row_ref, grads_ref, index_out, ids_out, *rest):
    outs = rest[: len(ks)]
    onehot_ref, value_ref, rank_ref, index_smem, grads_vmem, owner_vmem, row_vmem, sem, sem2, sem3 = rest[len(ks) :]
    load_owner = pltpu.make_async_copy(owner_ref, owner_vmem, sem2)
    load_row = pltpu.make_async_copy(row_ref, row_vmem, sem3)
    load = pltpu.make_async_copy(grads_ref, grads_vmem, sem)
    load_owner.start()
    load_row.start()
    load.start()
    load_owner.wait()
    load_row.wait()
    me = lax.axis_index("grp") * n_dev + lax.axis_index("dev")
    blocks = owner_ref.shape[0]
    id_rows = id_rows_of(slots)
    owner_at = lax.broadcasted_iota(jnp.int32, (n, LANES), 0)
    slot_at = lax.broadcasted_iota(jnp.int32, (id_rows * LANES, LANES), 0)
    lane = lax.broadcasted_iota(jnp.int32, (1, LANES), 1)
    upper = (
        lax.broadcasted_iota(jnp.int32, (LANES, LANES), 0)
        <= lax.broadcasted_iota(jnp.int32, (LANES, LANES), 1)
    ).astype(jnp.bfloat16)
    partner = owner_vmem[...] ^ me
    for r in range(blocks):
        hit = owner_at == partner[r : r + 1, :]
        onehot_ref[r * n : (r + 1) * n, :] = hit.astype(jnp.float32).astype(jnp.bfloat16)
    inclusive = jnp.dot(onehot_ref[...], upper, preferred_element_type=jnp.float32)
    base = jnp.full((n, 1), -1.0, jnp.float32)
    row1 = row_vmem[...] + 1
    for r in range(blocks):
        hit = owner_at == partner[r : r + 1, :]
        counts = inclusive[r * n : (r + 1) * n, :]
        rank = jnp.sum(jnp.where(hit, counts + base, 0.0), axis=0, keepdims=True).astype(jnp.int32)
        base = base + counts[:, LANES - 1 :]
        cols = slice(r * LANES, (r + 1) * LANES)
        rank_ref[:, cols] = (slot_at == rank).astype(jnp.float32).astype(jnp.bfloat16)
        source = lane + r * LANES
        parts = (source >> 6, source & 63, row1[r : r + 1, :] >> 7, row1[r : r + 1, :] & 127)
        for p, part in enumerate(parts):
            value_ref[p * n : (p + 1) * n, cols] = jnp.where(hit, part.astype(jnp.float32), 0.0).astype(jnp.bfloat16)
    found = lax.dot_general(
        value_ref[...], rank_ref[...], (((1,), (1,)), ((), ())), preferred_element_type=jnp.float32
    )
    index = (found[:n] * 64.0 + found[n : 2 * n]).astype(jnp.int32)
    ids = found[2 * n : 3 * n] * 128.0 + found[3 * n :]
    ids = jnp.where(ids == 0.0, float(rows_dev), ids - 1.0)
    for q in range(id_rows):
        index_out[q * n : (q + 1) * n, :] = index[:, q * LANES : (q + 1) * LANES]
        ids_out[q * n : (q + 1) * n, :] = ids[:, q * LANES : (q + 1) * LANES]
    to_smem = pltpu.make_async_copy(index_out, index_smem, sem2)
    to_smem.start()
    to_smem.wait()
    load.wait()
    for k, out in zip(ks, outs):
        for j in range(slots):
            source_row = index_smem[j // LANES * n + k, j % LANES]
            out[j] = grads_vmem[pl.ds(source_row, 1), :]
        for q in range(id_rows):
            out[slots + q] = ids_out[q * n + k : q * n + k + 1, :]


def pack_kernel(n, slots, messages, passed, index_ref, ids_ref, grads_ref, *refs):
    passed_ref = None
    if passed:
        passed_ref, *refs = refs
    outs, refs = refs[: len(messages)], refs[len(messages) :]
    grads_vmem, *bufs, sem, pass_sem, out_sem = refs
    rows = slots + id_rows_of(slots)
    load = pltpu.make_async_copy(grads_ref, grads_vmem, sem)
    load.start()
    loads = []
    for m, parts in enumerate(messages):
        loads.append([])
        for p, (kind, i) in enumerate(parts):
            if kind == "pass":
                copy = pltpu.make_async_copy(
                    passed_ref.at[pl.ds(i * rows, rows)], bufs[m].at[pl.ds(p * rows, rows)], pass_sem.at[m]
                )
                copy.start()
                loads[m].append(copy)
    load.wait()
    step = min(UNROLL, slots)
    stores = []
    for m, parts in enumerate(messages):
        buf = bufs[m]
        for p, (kind, k) in enumerate(parts):
            if kind == "pass":
                continue
            for q in range(id_rows_of(slots)):

                def body(it, carry, q=q, k=k, base=p * rows + q * LANES):
                    for u in range(step):
                        j = it * step + u
                        source_row = index_ref[(q * n + k) * LANES + j]
                        buf[base + j] = grads_vmem[pl.ds(source_row, 1), :]
                    return carry

                lax.fori_loop(0, min(slots, LANES) // step, body, 0)
                buf[p * rows + slots + q] = ids_ref[q * n + k : q * n + k + 1, :]
        for copy in loads[m]:
            copy.wait()
        store = pltpu.make_async_copy(buf, outs[m], out_sem.at[m])
        store.start()
        stores.append(store)
    for store in stores:
        store.wait()


def block_shape(slots, width):
    return (slots + id_rows_of(slots), 1, width)


def plan(n, n_dev, slots, rows_dev, ks, owner, row, grads):
    count, width = grads.shape
    rows = id_rows_of(slots) * n
    return pl.pallas_call(
        functools.partial(plan_kernel, n, n_dev, slots, rows_dev, ks),
        out_shape=[
            jax.ShapeDtypeStruct((rows, LANES), jnp.int32),
            jax.ShapeDtypeStruct((rows, LANES), jnp.float32),
        ]
        + [jax.ShapeDtypeStruct(block_shape(slots, width), jnp.float32)] * len(ks),
        in_specs=[HBM, HBM, HBM],
        out_specs=[VMEM] * (2 + len(ks)),
        scratch_shapes=[
            pltpu.VMEM((count // LANES * n, LANES), jnp.bfloat16),
            pltpu.VMEM((4 * n, count), jnp.bfloat16),
            pltpu.VMEM((id_rows_of(slots) * LANES, count), jnp.bfloat16),
            pltpu.SMEM((rows, LANES), jnp.int32),
            pltpu.VMEM((count, width), jnp.float32),
            pltpu.VMEM((count // LANES, LANES), jnp.int32),
            pltpu.VMEM((count // LANES, LANES), jnp.int32),
            pltpu.SemaphoreType.DMA,
            pltpu.SemaphoreType.DMA,
            pltpu.SemaphoreType.DMA,
        ],
        compiler_params=pltpu.CompilerParams(vmem_limit_bytes=32 * MIB),
        name="plan",
    )(in_hbm(owner.reshape(count // LANES, LANES)), in_hbm(row.reshape(count // LANES, LANES)), in_hbm(grads))


def pack(n, slots, messages, index, ids, grads, passed=None):
    rows, one, width = block_shape(slots, grads.shape[1])
    return pl.pallas_call(
        functools.partial(pack_kernel, n, slots, messages, passed is not None),
        out_shape=[pltpu.HBM((rows * len(message), one, width), jnp.float32) for message in messages],
        in_specs=[SMEM, VMEM, HBM] + ([HBM] if passed is not None else []),
        out_specs=[HBM] * len(messages),
        scratch_shapes=[pltpu.VMEM(grads.shape, jnp.float32)]
        + [pltpu.VMEM((rows * len(message), one, width), jnp.float32) for message in messages]
        + [pltpu.SemaphoreType.DMA, pltpu.SemaphoreType.DMA((len(messages),)), pltpu.SemaphoreType.DMA((len(messages),))],
        compiler_params=pltpu.CompilerParams(vmem_limit_bytes=16 * MIB),
        name="pack",
    )(index.reshape(-1), ids, in_hbm(grads), *([passed] if passed is not None else []))


def add_rows(accs, row_of, id_of, count):
    ways = len(accs)
    step = min(UNROLL, count)

    def body(it, carry):
        for u0 in range(0, step, ways):
            at = [it * step + u0 + a for a in range(ways)]
            ids = [id_of(j) for j in at]
            sums = [acc[pl.ds(i, 1), :] - LEARN * row_of(j) for acc, i, j in zip(accs, ids, at)]
            for acc, i, s in zip(accs, ids, sums):
                acc[pl.ds(i, 1), :] = s
        return carry

    lax.fori_loop(0, count // step, body, 0)


def apply_kernel(slots, n_blocks, n_hot, ways, first, last, pieces, *refs):
    table_ref = None
    if first:
        table_ref, *refs = refs
    else:
        refs = refs[ways:]
    blocks, refs = refs[:n_blocks], refs[n_blocks:]
    hot_ids_ref, hots = None, ()
    if n_hot:
        hot_ids_ref, *refs = refs
        hots, refs = refs[:n_hot], refs[n_hot:]
    accs, refs = refs[:ways], refs[ways:]
    out_ref = None
    if last:
        out_ref, *refs = refs
    ids_vmem, ids_smem, sem, table_sem, out_sem = refs
    id_rows = id_rows_of(slots)
    rows_dev = accs[0].shape[0] - 8
    if first:
        load = pltpu.make_async_copy(table_ref, accs[0].at[pl.ds(0, rows_dev)], table_sem)
        load.start()
    moves = []
    height = slots + id_rows
    parts = [(blk, base) for blk in blocks for base in range(0, blk.shape[0], height)]
    for b, (blk, base) in enumerate(parts):
        for q in range(id_rows):
            at = b * id_rows + q
            ids_vmem[at] = blk[base + slots + q].astype(jnp.int32)
            move = pltpu.make_async_copy(ids_vmem.at[at, 0], ids_smem.at[pl.ds(at * LANES, LANES)], sem)
            move.start()
            moves.append(move)
    chunk = 64
    if first:

        def clear(it, carry):
            for acc in accs[1:]:
                acc[pl.ds(it * chunk, chunk), :] = jnp.zeros((chunk, LANES), jnp.float32)
            return carry

        lax.fori_loop(0, rows_dev // chunk, clear, 0)
        load.wait()
    for move in moves:
        move.wait()
    for b, (blk, base) in enumerate(parts):
        for q in range(id_rows):
            add_rows(
                accs,
                lambda j, blk=blk, base=base, q=q: blk[base + q * LANES + j],
                lambda j, at=b * id_rows + q: ids_smem[at * LANES + j],
                min(slots, LANES),
            )
    mine = 2 * lax.axis_index("grp") + lax.axis_index("dev") % 2
    start = (lax.axis_index("grp") * lax.axis_size("dev") + lax.axis_index("dev")) * rows_dev
    for at in range(2 * n_hot):
        hot = hots[at // 2]
        part = hot.shape[0] // 2

        def target(j, base=(mine ^ at) * part):
            local = hot_ids_ref[base + j] - start
            return jnp.where((local >= 0) & (local < rows_dev), local, rows_dev)

        add_rows(accs, lambda j, hot=hot, base=at % 2 * part: hot[pl.ds(base + j, 1), :], target, part)
    if not last:
        return
    piece = rows_dev // pieces
    stores = []
    for p in range(pieces):

        def combine(it, carry, p=p):
            rows = pl.ds(p * piece + it * chunk, chunk)
            total = accs[0][rows, :]
            for acc in accs[1:]:
                total = total + acc[rows, :]
            accs[0][rows, :] = total
            return carry

        lax.fori_loop(0, piece // chunk, combine, 0)
        rows = pl.ds(p * piece, piece)
        store = pltpu.make_async_copy(accs[0].at[rows], out_ref.at[rows], out_sem.at[p])
        store.start()
        stores.append(store)
    for store in stores:
        store.wait()


def apply_blocks(slots, table, accs, blocks, hot_ids, hots, last):
    ways, pieces = WAYS, 8
    first = accs is None
    if first:
        rows_dev, width = table.shape
    else:
        rows_dev, width = accs[0].shape[0] - 8, accs[0].shape[1]
    id_rows = id_rows_of(slots)
    hot_args = [hot_ids, *hots] if hots else []
    n_parts = sum(block.shape[0] for block in blocks) // (slots + id_rows)
    outs = pl.pallas_call(
        functools.partial(apply_kernel, slots, len(blocks), len(hots), ways, first, last, pieces),
        out_shape=[pltpu.VMEM((rows_dev + 8, width), jnp.float32)] * ways
        + ([pltpu.HBM((rows_dev, width), jnp.float32)] if last else []),
        in_specs=([HBM] if first else [VMEM] * ways)
        + [VMEM] * len(blocks)
        + ([SMEM] + [VMEM] * len(hots) if hots else []),
        out_specs=[VMEM] * ways + ([HBM] if last else []),
        scratch_shapes=[
            pltpu.VMEM((n_parts * id_rows, 1, LANES), jnp.int32),
            pltpu.SMEM((n_parts * id_rows * LANES,), jnp.int32),
            pltpu.SemaphoreType.DMA,
            pltpu.SemaphoreType.DMA,
            pltpu.SemaphoreType.DMA((pieces,)),
        ],
        input_output_aliases={} if first else {w: w for w in range(ways)},
        compiler_params=pltpu.CompilerParams(vmem_limit_bytes=24 * MIB),
        name="apply",
    )(*([in_hbm(table)] if first else accs), *blocks, *hot_args)
    return outs[ways] if last else outs


def sum_kernel(*refs):
    *parts, out_ref = refs
    total = parts[0][...]
    for part in parts[1:]:
        total = total + part[...]
    out_ref[...] = total


def join_kernel(a_ref, b_ref, out_ref):
    half = a_ref.shape[0]
    out_ref[:half, :] = a_ref[...]
    out_ref[half:, :] = b_ref[...]


def small_call(kernel, shape, *args):
    return pl.pallas_call(
        kernel,
        out_shape=jax.ShapeDtypeStruct(shape, jnp.float32),
        in_specs=[VMEM] * len(args),
        out_specs=VMEM,
        compiler_params=pltpu.CompilerParams(vmem_limit_bytes=4 * MIB),
    )(*args)


def swap(x, axis, size, k):
    return lax.ppermute(x, axis, [(s, s ^ k) for s in range(size)])


def scatter_share(x, axis, size, step):
    part = x.shape[0] // size
    mine = lax.axis_index(axis) // step % size
    share = lax.dynamic_slice_in_dim(x, mine * part, part, 0)
    full = lax.axis_size(axis)
    for k in range(1, size):
        share = share + swap(lax.dynamic_slice_in_dim(x, (mine ^ k) * part, part, 0), axis, full, k * step)
    return share


def partner_order(n, n_dev):
    per_grp = n_dev // 2
    near, cross = [], []
    for start in range(0, n // 2, per_grp):
        chips = range(start, start + per_grp)
        near.append([c for c in chips if c and not c & (per_grp // 2)])
        cross.append([c for c in chips if c & (per_grp // 2)])
    return near, cross


def cores_of(chips):
    return [k for c in chips for k in (2 * c, 2 * c + 1)]


def on_device(table, cold_grads, cold_owner, cold_row, hot_grads, hot_slot, hot_ids):
    n_grp = lax.axis_size("grp")
    n_dev = lax.axis_size("dev")
    n = n_grp * n_dev
    rows_dev = table.shape[0]
    hot = hot_ids.shape[0]
    slots = max(4, 2 * cold_grads.shape[0] // n)
    near, cross = partner_order(n, n_dev)
    first, second = cores_of(cross[0]), cores_of(near[1] + cross[1] + near[2])
    rest = cross[2] + near[0] + near[3] + cross[3] + [0]
    index, ids, *blocks = plan(n, n_dev, slots, rows_dev, first, cold_owner[:, 0], cold_row, cold_grads)
    blocks += pack(n, slots, [[("own", k)] for k in second], index, ids, cold_grads)
    head = []
    for k, block in zip(first + second, blocks):
        head.append(swap(block, AXES, n, k))
    (passed,) = pack(n, slots, [[("own", 2 * c + 1) for c in rest]], index, ids, cold_grads)
    passed = swap(passed, "dev", n_dev, 1)
    messages = [[("own", 2 * c), ("pass", i)] for i, c in enumerate(rest)]
    *packed, own = pack(n, slots, messages, index, ids, cold_grads, passed)
    arrived = {}
    for c, message in zip(rest, packed):
        arrived[c] = swap(message, AXES, n, 2 * c)

    pick = (jnp.arange(hot, dtype=jnp.int32)[:, None] == hot_slot[None, :]).astype(jnp.float32)
    partial_sum = jnp.dot(
        pick, hot_grads, precision=lax.Precision.HIGHEST, preferred_element_type=jnp.float32
    )
    share = scatter_share(partial_sum, "grp", n_grp, 1)
    share = scatter_share(share, "dev", 2, 1)
    others = [swap(share, "dev", n_dev, 2 * k) for k in range(1, n_dev // 2)]
    whole = small_call(sum_kernel, share.shape, share, *others)
    other = swap(whole, "dev", n_dev, 1)
    whole = small_call(join_kernel, (2 * share.shape[0], share.shape[1]), whole, other)
    hots = [whole] + [swap(whole, "grp", n_grp, k) for k in range(1, n_grp)]
    accs = apply_blocks(slots, table, None, head + [own], None, [], False)
    accs = apply_blocks(slots, None, accs, [arrived[c] for c in near[0] + near[3]], None, [], False)
    accs = apply_blocks(slots, None, accs, [arrived[c] for c in cross[2]], None, [], False)
    accs = apply_blocks(slots, None, accs, [arrived[c] for c in cross[3][:-1]], None, [], False)
    return apply_blocks(slots, None, accs, [arrived[cross[3][-1]]], hot_ids, hots, True)


def solution(mesh):
    in_specs = (
        P(AXES, None),
        P(AXES, None),
        P(AXES, None),
        P(AXES),
        P(AXES, None),
        P(AXES),
        P(),
    )

    return jax.shard_map(on_device, mesh=mesh, in_specs=in_specs, out_specs=P(AXES, None), check_vma=False)
```

profile of v0, /device:TPU:8, one launch (start us, length us, event | category | flops | bytes accessed | tf_op | source)
XLA Modules:
  0.0 164.6 jit_solution(17744750569784753369)
XLA Ops:
  0.0 4.1 %plan.1 = (s32[64,128]{1,0:T(8,128)S(1)}, f32[64,128]{1,0:T(8,128)S(1)}, f32[258,1,128]{2,1,0:T(1,128)S(1)}, f32[258,1,128]{2,1,0:T(1,128)S(1)}, f32[258,1,128]{2,1,0:T(1,128)S(1)}, /*index=5*/f32[258,1,128]{2,1,0:T(1,128)S(1)}) custom-call(s32[32,128]{1,0:T(8,128)} %bitcast.7, s32[32,128]{1,0:T(8,128)} %bitcast.8, f32[4096,128]{1,0:T(8,128)} %grads_ref.7), custom_call_target="tpu_custom_call" | custom-call | tf_op jit(solution)/shard_map/plan/pallas_call | solution.py:145
  4.2 5.5 %pack.4 = f32[2064,1,128]{2,1,0:T(1,128)} custom-call(s32[8192]{0:T(1024)S(1)} %bitcast.4, f32[64,128]{1,0:T(8,128)S(1)} %get-tuple-element.53.ids_ref, f32[4096,128]{1,0:T(8,128)} %grads_ref.7), custom_call_target="tpu_custom_call" | custom-call | tf_op jit(solution)/shard_map/pack/pallas_call | solution.py:173
  9.7 0.1 collective-permute-start.16
  9.8 0.7 fusion
  10.5 1.6 collective-permute-start.24
  12.1 1.5 collective-permute-start.26
  13.6 0.5 collective-permute-start.25
  14.1 0.4 collective-permute-done.24
  14.5 2.4 %collective-permute-done.26 = f32[64,128]{1,0:T(8,128)S(1)} collective-permute-done((f32[64,128]{1,0:T(8,128)S(1)}, f32[64,128]{1,0:T(8,128)S(1)}, u32[]{:S(2)}, u32[]{:S(2)}) %collective-permute-start.26) | collective-permute-done | bytes 32800 | tf_op jit(solution)/shard_map/ppermute | solution.py:344
  16.9 0.6 collective-permute-done.25
  17.5 0.1 collective-permute-start.27
  17.6 2.7 %collective-permute-start = (f32[258,1,128]{2,1,0:T(1,128)S(1)}, f32[258,1,128]{2,1,0:T(1,128)S(1)}, u32[]{:S(2)}, u32[]{:S(2)}) collective-permute-start(f32[258,1,128]{2,1,0:T(1,128)S(1)} %get-tuple-element.48), channel_id=1, source_target_pairs={{0,4},{1,5},{2,6},{3,7},{4,0},{5,1},{6,2},{7,3},{8,12},{9,13},{10,... | collective-permute-start | bytes 396296 | tf_op jit(solution)/shard_map/ppermute | solution.py:344
  20.3 0.1 collective-permute-start.1
  20.4 1.6 collective-permute-start.30
  22.0 1.2 collective-permute-start.29
  23.3 9.9 %collective-permute-done.30.refs_3_ = f32[32,128]{1,0:T(8,128)S(1)} collective-permute-done((f32[32,128]{1,0:T(8,128)S(1)}, f32[32,128]{1,0:T(8,128)S(1)}, u32[]{:S(2)}, u32[]{:S(2)}) %collective-permute-start.30) | collective-permute-done | bytes 16416 | tf_op jit(solution)/shard_map/ppermute | solution.py:344
  33.2 0.0 collective-permute-start.28
  33.2 0.3 collective-permute-done.29.refs_2_
  33.5 3.4 %collective-permute-done.28.refs_1_ = f32[32,128]{1,0:T(8,128)S(1)} collective-permute-done((f32[32,128]{1,0:T(8,128)S(1)}, f32[32,128]{1,0:T(8,128)S(1)}, u32[]{:S(2)}, u32[]{:S(2)}) %collective-permute-start.28) | collective-permute-done | bytes 16416 | tf_op jit(solution)/shard_map/ppermute | solution.py:344
  36.9 2.5 %collective-permute-start.2 = (f32[258,1,128]{2,1,0:T(1,128)S(1)}, f32[258,1,128]{2,1,0:T(1,128)S(1)}, u32[]{:S(2)}, u32[]{:S(2)}) collective-permute-start(f32[258,1,128]{2,1,0:T(1,128)S(1)} %get-tuple-element.50), channel_id=1, source_target_pairs={{0,6},{1,7},{2,4},{3,5},{4,2},{5,3},{6,0},{7,1},{8,14},{9,15},{10,... | collective-permute-start | bytes 396296 | tf_op jit(solution)/shard_map/ppermute | solution.py:344
  39.4 0.9 collective-permute-start.3
  40.3 6.4 %pack.3 = (f32[258,1,128]{2,1,0:T(1,128)}, f32[258,1,128]{2,1,0:T(1,128)}, f32[258,1,128]{2,1,0:T(1,128)}, f32[258,1,128]{2,1,0:T(1,128)}, f32[258,1,128]{2,1,0:...) custom-call(s32[8192]{0:T(1024)S(1)} %bitcast.5, ...), custom_call_target="tpu_custom_call" | custom-call | tf_op jit(solution)/shard_map/pack/pallas_call | solution.py:173
  46.7 1.6 collective-permute-start.4
  48.3 0.2 collective-permute-start.5
  48.5 0.4 collective-permute-done.2.refs_3_
  48.9 1.4 collective-permute-start.6
  50.3 1.3 collective-permute-done.3.refs_4_
  51.6 0.0 collective-permute-start.7
  51.6 7.4 %collective-permute-done.4.refs_5_ = f32[258,1,128]{2,1,0:T(1,128)S(1)} collective-permute-done((f32[258,1,128]{2,1,0:T(1,128)}, f32[258,1,128]{2,1,0:T(1,128)S(1)}, u32[]{:S(2)}, u32[]{:S(2)}) %collective-permute-start.4) | collective-permute-done | bytes 132128 | tf_op jit(solution)/shard_map/ppermute | solution.py:344
  59.0 4.5 %collective-permute-start.8 = (f32[258,1,128]{2,1,0:T(1,128)}, f32[258,1,128]{2,1,0:T(1,128)S(1)}, u32[]{:S(2)}, u32[]{:S(2)}) collective-permute-start(f32[258,1,128]{2,1,0:T(1,128)} %get-tuple-element.58), channel_id=1, source_target_pairs={{0,12},{1,13},{2,14},{3,15},{4,8},{5,9},{6,10},{7,11},{8,4},{9,5},... | collective-permute-start | bytes 396296 | tf_op jit(solution)/shard_map/ppermute | solution.py:344
  63.5 1.6 collective-permute-start.9
  65.2 0.2 collective-permute-start.10
  65.3 0.0 collective-permute-done.7.refs_8_
  65.4 2.1 %collective-permute-start.11 = (f32[258,1,128]{2,1,0:T(1,128)}, f32[258,1,128]{2,1,0:T(1,128)S(1)}, u32[]{:S(2)}, u32[]{:S(2)}) collective-permute-start(f32[258,1,128]{2,1,0:T(1,128)} %get-tuple-element.61), channel_id=1, source_target_pairs={{0,15},{1,14},{2,13},{3,12},{4,11},{5,10},{6,9},{7,8},{8,7},{9,6},... | collective-permute-start | bytes 396296 | tf_op jit(solution)/shard_map/ppermute | solution.py:344
  67.5 0.0 collective-permute-done.16.refs_0_
  67.5 0.5 collective-permute-start.12
  68.0 5.4 %pack.5 = (f32[516,1,128]{2,1,0:T(1,128)}, f32[516,1,128]{2,1,0:T(1,128)}, f32[516,1,128]{2,1,0:T(1,128)}, f32[516,1,128]{2,1,0:T(1,128)}, f32[516,1,128]{2,1,0:...) custom-call(s32[8192]{0:T(1024)S(1)} %bitcast.6, ...), custom_call_target="tpu_custom_call" | custom-call | tf_op jit(solution)/shard_map/pack/pallas_call | solution.py:173
  73.4 2.0 %collective-permute-done.8.refs_9_ = f32[258,1,128]{2,1,0:T(1,128)S(1)} collective-permute-done((f32[258,1,128]{2,1,0:T(1,128)}, f32[258,1,128]{2,1,0:T(1,128)S(1)}, u32[]{:S(2)}, u32[]{:S(2)}) %collective-permute-start.8) | collective-permute-done | bytes 132128 | tf_op jit(solution)/shard_map/ppermute | solution.py:344
  75.5 3.9 %collective-permute-start.17 = (f32[516,1,128]{2,1,0:T(1,128)}, f32[516,1,128]{2,1,0:T(1,128)S(1)}, u32[]{:S(2)}, u32[]{:S(2)}) collective-permute-start(f32[516,1,128]{2,1,0:T(1,128)} %get-tuple-element.71), channel_id=1, source_target_pairs={{0,2},{1,3},{2,0},{3,1},{4,6},{5,7},{6,4},{7,5},{8,10},{9,11},{10,... | collective-permute-start | bytes 792584 | tf_op jit(solution)/shard_map/ppermute | solution.py:344
  79.4 0.0 collective-permute-done.9.refs_10_
  79.4 0.4 collective-permute-start.18
  79.8 3.9 %collective-permute-done.10.refs_11_ = f32[258,1,128]{2,1,0:T(1,128)S(1)} collective-permute-done((f32[258,1,128]{2,1,0:T(1,128)}, f32[258,1,128]{2,1,0:T(1,128)S(1)}, u32[]{:S(2)}, u32[]{:S(2)}) %collective-permute-start.10) | collective-permute-done | bytes 132128 | tf_op jit(solution)/shard_map/ppermute | solution.py:344
  83.7 0.2 collective-permute-done.11.refs_12_
  83.9 3.6 %collective-permute-start.15 = (f32[258,1,128]{2,1,0:T(1,128)}, f32[258,1,128]{2,1,0:T(1,128)S(1)}, u32[]{:S(2)}, u32[]{:S(2)}) collective-permute-start(f32[258,1,128]{2,1,0:T(1,128)} %get-tuple-element.65), channel_id=1, source_target_pairs={{0,19},{1,18},{2,17},{3,16},{4,23},{5,22},{6,21},{7,20},{8,27},{9,... | collective-permute-start | bytes 396296 | tf_op jit(solution)/shard_map/ppermute | solution.py:344
  87.5 11.4 %collective-permute-done.13.refs_14_ = f32[258,1,128]{2,1,0:T(1,128)S(1)} collective-permute-done((f32[258,1,128]{2,1,0:T(1,128)}, f32[258,1,128]{2,1,0:T(1,128)S(1)}, u32[]{:S(2)}, u32[]{:S(2)}) %collective-permute-start.13) | collective-permute-done | bytes 132128 | tf_op jit(solution)/shard_map/ppermute | solution.py:344
  98.9 0.0 collective-permute-done.14.refs_15_
  98.9 3.8 %collective-permute-start.20 = (f32[516,1,128]{2,1,0:T(1,128)}, f32[516,1,128]{2,1,0:T(1,128)S(1)}, u32[]{:S(2)}, u32[]{:S(2)}) collective-permute-start(f32[516,1,128]{2,1,0:T(1,128)} %get-tuple-element.78), channel_id=1, source_target_pairs={{0,20},{1,21},{2,22},{3,23},{4,16},{5,17},{6,18},{7,19},{8,28},{9,... | collective-permute-start | bytes 792584 | tf_op jit(solution)/shard_map/ppermute | solution.py:344
  102.8 1.9 %collective-permute-start.21 = (f32[516,1,128]{2,1,0:T(1,128)}, f32[516,1,128]{2,1,0:T(1,128)S(1)}, u32[]{:S(2)}, u32[]{:S(2)}) collective-permute-start(f32[516,1,128]{2,1,0:T(1,128)} %get-tuple-element.79), channel_id=1, source_target_pairs={{0,22},{1,23},{2,20},{3,21},{4,18},{5,19},{6,16},{7,17},{8,30},{9,... | collective-permute-start | bytes 792584 | tf_op jit(solution)/shard_map/ppermute | solution.py:344
  104.7 0.0 collective-permute-done.17.refs_4_
  104.7 1.4 collective-permute-start.22
  106.0 1.5 collective-permute-start.23
  107.6 2.6 %collective-permute-done.19.refs_6_ = f32[516,1,128]{2,1,0:T(1,128)S(1)} collective-permute-done((f32[516,1,128]{2,1,0:T(1,128)}, f32[516,1,128]{2,1,0:T(1,128)S(1)}, u32[]{:S(2)}, u32[]{:S(2)}) %collective-permute-start.19) | collective-permute-done | bytes 264224 | tf_op jit(solution)/shard_map/ppermute | solution.py:344
  110.2 2.5 %collective-permute-start.34 = (f32[64,128]{1,0:T(8,128)S(1)}, f32[64,128]{1,0:T(8,128)S(1)}, u32[]{:S(2)}, u32[]{:S(2)}) collective-permute-start(f32[64,128]{1,0:T(8,128)S(1)} %shard_map.74.refs_6_), channel_id=1, source_target_pairs={{0,24},{8,16},{16,8},{24,0},{1,25},{9,17},{17,9},{25,1},{2,26},{10... | collective-permute-start | bytes 98312 | tf_op jit(solution)/shard_map/ppermute | solution.py:344
  112.7 20.4 %collective-permute-done.20.refs_4_ = f32[516,1,128]{2,1,0:T(1,128)S(1)} collective-permute-done((f32[516,1,128]{2,1,0:T(1,128)}, f32[516,1,128]{2,1,0:T(1,128)S(1)}, u32[]{:S(2)}, u32[]{:S(2)}) %collective-permute-start.20) | collective-permute-done | bytes 264224 | tf_op jit(solution)/shard_map/ppermute | solution.py:344
  133.1 0.1 collective-permute-start.33
  133.2 7.6 %collective-permute-done.21.refs_5_ = f32[516,1,128]{2,1,0:T(1,128)S(1)} collective-permute-done((f32[516,1,128]{2,1,0:T(1,128)}, f32[516,1,128]{2,1,0:T(1,128)S(1)}, u32[]{:S(2)}, u32[]{:S(2)}) %collective-permute-start.21) | collective-permute-done | bytes 264224 | tf_op jit(solution)/shard_map/ppermute | solution.py:344
  140.8 0.8 collective-permute-start.32
  141.6 0.9 copy-done.1
  142.6 10.1 %apply.5 = (f32[8200,128]{1,0:T(8,128)S(1)}, f32[8200,128]{1,0:T(8,128)S(1)}, f32[8200,128]{1,0:T(8,128)S(1)}, f32[8200,128]{1,0:T(8,128)S(1)}) custom-call(f32[8192,128]{1,0:T(8,128)} %refs_0_.1, f32[258,1,128]{2,1,0:T(1,128)S(1)} %collective-permute-done.refs_1_, f32[258,1,128]{2,1,0:T(1,128)S(1)} %collective-permute-done.1.refs_2_, ...), custom_call_target="tpu_custom_call" | custom-call | tf_op jit(solution)/shard_map/apply/pallas_call | solution.py:297
  152.7 3.1 %apply.6 = (f32[8200,128]{1,0:T(8,128)S(1)}, f32[8200,128]{1,0:T(8,128)S(1)}, f32[8200,128]{1,0:T(8,128)S(1)}, f32[8200,128]{1,0:T(8,128)S(1)}) custom-call(f32[8200,128]{1,0:T(8,128)S(1)} %get-tuple-element.67.refs_0_, f32[8200,128]{1,0:T(8,128)S(1)} %get-tuple-element.68.refs_1_, ...), custom_call_target="tpu_custom_call", output_to_operand_aliasing={{0}: (0, {}), {1}: (1, {}), {2}: (2, {}), {3}: (3, {})} | custom-call | tf_op jit(solution)/shard_map/apply/pallas_call | solution.py:297
  155.7 2.3 %apply.7 = (f32[8200,128]{1,0:T(8,128)S(1)}, f32[8200,128]{1,0:T(8,128)S(1)}, f32[8200,128]{1,0:T(8,128)S(1)}, f32[8200,128]{1,0:T(8,128)S(1)}) custom-call(f32[8200,128]{1,0:T(8,128)S(1)} %get-tuple-element.74.refs_0_, f32[8200,128]{1,0:T(8,128)S(1)} %get-tuple-element.75.refs_1_, ...), custom_call_target="tpu_custom_call", output_to_operand_aliasing={{0}: (0, {}), {1}: (1, {}), {2}: (2, {}), {3}: (3, {})} | custom-call | tf_op jit(solution)/shard_map/apply/pallas_call | solution.py:297
  158.1 0.0 copy-start.2
  158.1 1.4 apply.8
  159.6 5.1 %apply.9 = (f32[8200,128]{1,0:T(8,128)S(1)}, f32[8200,128]{1,0:T(8,128)S(1)}, f32[8200,128]{1,0:T(8,128)S(1)}, f32[8200,128]{1,0:T(8,128)S(1)}, f32[8192,128]{1,0:T(8,128)}) custom-call(f32[8200,128]{1,0:T(8,128)S(1)} %get-tuple-element.85.refs_0_, ...), custom_call_target="tpu_custom_call", output_to_operand_aliasing={{0}: (0, {}), {1}: (1, {}), {2}: (2, {}), {3}: (3, {})} | custom-call | tf_op jit(solution)/shard_map/apply/pallas_call | solution.py:297
  (30 shorter events, 0.1 us)
Async XLA Ops:
  0.0 9.8 %copy-start = (f32[1024,128]{1,0:T(8,128)S(1)}, f32[1024,128]{1,0:T(8,128)}, u32[]{:S(2)}) copy-start(f32[1024,128]{1,0:T(8,128)} %param.11) | copy-start | bytes 1572868
  0.0 9.8 %copy-start.3 = (s32[1024]{0:T(1024)S(1)}, s32[1024]{0:T(1024)}, u32[]{:S(2)}) copy-start(s32[1024]{0:T(1024)} %param.12) | copy-start | bytes 12292
  9.7 57.8 %collective-permute-start.16 = (f32[2064,1,128]{2,1,0:T(1,128)}, f32[2064,1,128]{2,1,0:T(1,128)S(1)}, u32[]{:S(2)}, u32[]{:S(2)}) collective-permute-start(f32[2064,1,128]{2,1,0:T(1,128)} %pack.4), channel_id=1, source_target_pairs={{0,1},{1,0},{2,3},{3,2},{4,5},{5,4},{6,7},{7,6},{8,9},{9,8},{10,11... | collective-permute-start | bytes 3170312 | tf_op jit(solution)/shard_map/ppermute | solution.py:344
  10.5 4.0 %collective-permute-start.24 = (f32[64,128]{1,0:T(8,128)S(1)}, f32[64,128]{1,0:T(8,128)S(1)}, u32[]{:S(2)}, u32[]{:S(2)}) collective-permute-start(f32[64,128]{1,0:T(8,128)S(1)} %get-tuple-element.91), channel_id=1, source_target_pairs={{0,8},{8,0},{16,24},{24,16},{1,9},{9,1},{17,25},{25,17},{2,10},{10... | collective-permute-start | bytes 98312 | tf_op jit(solution)/shard_map/ppermute | solution.py:344
  12.1 4.8 %collective-permute-start.26 = (f32[64,128]{1,0:T(8,128)S(1)}, f32[64,128]{1,0:T(8,128)S(1)}, u32[]{:S(2)}, u32[]{:S(2)}) collective-permute-start(f32[64,128]{1,0:T(8,128)S(1)} %get-tuple-element.92), channel_id=1, source_target_pairs={{0,24},{8,16},{16,8},{24,0},{1,25},{9,17},{17,9},{25,1},{2,26},{10... | collective-permute-start | bytes 98312 | tf_op jit(solution)/shard_map/ppermute | solution.py:344
  13.6 3.9 %collective-permute-start.25 = (f32[64,128]{1,0:T(8,128)S(1)}, f32[64,128]{1,0:T(8,128)S(1)}, u32[]{:S(2)}, u32[]{:S(2)}) collective-permute-start(f32[64,128]{1,0:T(8,128)S(1)} %get-tuple-element.93), channel_id=1, source_target_pairs={{0,16},{8,24},{16,0},{24,8},{1,17},{9,25},{17,1},{25,9},{2,18},{10... | collective-permute-start | bytes 98312 | tf_op jit(solution)/shard_map/ppermute | solution.py:344
  17.5 2.8 %collective-permute-start.27 = (f32[32,128]{1,0:T(8,128)S(1)}, f32[32,128]{1,0:T(8,128)S(1)}, u32[]{:S(2)}, u32[]{:S(2)}) collective-permute-start(f32[32,128]{1,0:T(8,128)S(1)} %constant_dynamic-slice_fusion), channel_id=1, source_target_pairs={{0,1},{1,0},{2,3},{3,2},{4,5},{5,4},{6,7},{7,6},{8,9},{9,8},{10,11... | collective-permute-start | bytes 49160 | tf_op jit(solution)/shard_map/ppermute | solution.py:344
  17.6 29.1 %collective-permute-start = (f32[258,1,128]{2,1,0:T(1,128)S(1)}, f32[258,1,128]{2,1,0:T(1,128)S(1)}, u32[]{:S(2)}, u32[]{:S(2)}) collective-permute-start(f32[258,1,128]{2,1,0:T(1,128)S(1)} %get-tuple-element.48), channel_id=1, source_target_pairs={{0,4},{1,5},{2,6},{3,7},{4,0},{5,1},{6,2},{7,3},{8,12},{9,13},{10,... | collective-permute-start | bytes 396296 | tf_op jit(solution)/shard_map/ppermute | solution.py:344
  20.3 28.0 %collective-permute-start.1 = (f32[258,1,128]{2,1,0:T(1,128)S(1)}, f32[258,1,128]{2,1,0:T(1,128)S(1)}, u32[]{:S(2)}, u32[]{:S(2)}) collective-permute-start(f32[258,1,128]{2,1,0:T(1,128)S(1)} %get-tuple-element.49), channel_id=1, source_target_pairs={{0,5},{1,4},{2,7},{3,6},{4,1},{5,0},{6,3},{7,2},{8,13},{9,12},{10,... | collective-permute-start | bytes 396296 | tf_op jit(solution)/shard_map/ppermute | solution.py:344
  20.4 12.8 %collective-permute-start.30 = (f32[32,128]{1,0:T(8,128)S(1)}, f32[32,128]{1,0:T(8,128)S(1)}, u32[]{:S(2)}, u32[]{:S(2)}) collective-permute-start(f32[32,128]{1,0:T(8,128)S(1)} %dynamic-slice_add_fusion.refs_0_), channel_id=1, source_target_pairs={{0,6},{1,7},{2,4},{3,5},{4,2},{5,3},{6,0},{7,1},{8,14},{9,15},{10,... | collective-permute-start | bytes 49160 | tf_op jit(solution)/shard_map/ppermute | solution.py:344
  22.0 11.4 %collective-permute-start.29 = (f32[32,128]{1,0:T(8,128)S(1)}, f32[32,128]{1,0:T(8,128)S(1)}, u32[]{:S(2)}, u32[]{:S(2)}) collective-permute-start(f32[32,128]{1,0:T(8,128)S(1)} %dynamic-slice_add_fusion.refs_0_), channel_id=1, source_target_pairs={{0,4},{1,5},{2,6},{3,7},{4,0},{5,1},{6,2},{7,3},{8,12},{9,13},{10,... | collective-permute-start | bytes 49160 | tf_op jit(solution)/shard_map/ppermute | solution.py:344
  33.2 3.7 %collective-permute-start.28 = (f32[32,128]{1,0:T(8,128)S(1)}, f32[32,128]{1,0:T(8,128)S(1)}, u32[]{:S(2)}, u32[]{:S(2)}) collective-permute-start(f32[32,128]{1,0:T(8,128)S(1)} %dynamic-slice_add_fusion.refs_0_), channel_id=1, source_target_pairs={{0,2},{1,3},{2,0},{3,1},{4,6},{5,7},{6,4},{7,5},{8,10},{9,11},{10,... | collective-permute-start | bytes 49160 | tf_op jit(solution)/shard_map/ppermute | solution.py:344
  36.9 2.5 %collective-permute-start.31 = (f32[32,128]{1,0:T(8,128)S(1)}, f32[32,128]{1,0:T(8,128)S(1)}, u32[]{:S(2)}, u32[]{:S(2)}) collective-permute-start(f32[32,128]{1,0:T(8,128)S(1)} %shard_map.73.a_ref), channel_id=1, source_target_pairs={{0,1},{1,0},{2,3},{3,2},{4,5},{5,4},{6,7},{7,6},{8,9},{9,8},{10,11... | collective-permute-start | bytes 49160 | tf_op jit(solution)/shard_map/ppermute | solution.py:344
  36.9 12.0 %collective-permute-start.2 = (f32[258,1,128]{2,1,0:T(1,128)S(1)}, f32[258,1,128]{2,1,0:T(1,128)S(1)}, u32[]{:S(2)}, u32[]{:S(2)}) collective-permute-start(f32[258,1,128]{2,1,0:T(1,128)S(1)} %get-tuple-element.50), channel_id=1, source_target_pairs={{0,6},{1,7},{2,4},{3,5},{4,2},{5,3},{6,0},{7,1},{8,14},{9,15},{10,... | collective-permute-start | bytes 396296 | tf_op jit(solution)/shard_map/ppermute | solution.py:344
  39.4 12.2 %collective-permute-start.3 = (f32[258,1,128]{2,1,0:T(1,128)S(1)}, f32[258,1,128]{2,1,0:T(1,128)S(1)}, u32[]{:S(2)}, u32[]{:S(2)}) collective-permute-start(f32[258,1,128]{2,1,0:T(1,128)S(1)} %get-tuple-element.51), channel_id=1, source_target_pairs={{0,7},{1,6},{2,5},{3,4},{4,3},{5,2},{6,1},{7,0},{8,15},{9,14},{10,... | collective-permute-start | bytes 396296 | tf_op jit(solution)/shard_map/ppermute | solution.py:344
  46.7 12.3 %collective-permute-start.4 = (f32[258,1,128]{2,1,0:T(1,128)}, f32[258,1,128]{2,1,0:T(1,128)S(1)}, u32[]{:S(2)}, u32[]{:S(2)}) collective-permute-start(f32[258,1,128]{2,1,0:T(1,128)} %get-tuple-element.54), channel_id=1, source_target_pairs={{0,8},{1,9},{2,10},{3,11},{4,12},{5,13},{6,14},{7,15},{8,0},{9,1},... | collective-permute-start | bytes 396296 | tf_op jit(solution)/shard_map/ppermute | solution.py:344
  48.3 15.3 %collective-permute-start.5 = (f32[258,1,128]{2,1,0:T(1,128)}, f32[258,1,128]{2,1,0:T(1,128)S(1)}, u32[]{:S(2)}, u32[]{:S(2)}) collective-permute-start(f32[258,1,128]{2,1,0:T(1,128)} %get-tuple-element.55), channel_id=1, source_target_pairs={{0,9},{1,8},{2,11},{3,10},{4,13},{5,12},{6,15},{7,14},{8,1},{9,0},... | collective-permute-start | bytes 396296 | tf_op jit(solution)/shard_map/ppermute | solution.py:344
  48.9 16.3 %collective-permute-start.6 = (f32[258,1,128]{2,1,0:T(1,128)}, f32[258,1,128]{2,1,0:T(1,128)S(1)}, u32[]{:S(2)}, u32[]{:S(2)}) collective-permute-start(f32[258,1,128]{2,1,0:T(1,128)} %get-tuple-element.56), channel_id=1, source_target_pairs={{0,10},{1,11},{2,8},{3,9},{4,14},{5,15},{6,12},{7,13},{8,2},{9,3},... | collective-permute-start | bytes 396296 | tf_op jit(solution)/shard_map/ppermute | solution.py:344
  51.6 13.7 %collective-permute-start.7 = (f32[258,1,128]{2,1,0:T(1,128)}, f32[258,1,128]{2,1,0:T(1,128)S(1)}, u32[]{:S(2)}, u32[]{:S(2)}) collective-permute-start(f32[258,1,128]{2,1,0:T(1,128)} %get-tuple-element.57), channel_id=1, source_target_pairs={{0,11},{1,10},{2,9},{3,8},{4,15},{5,14},{6,13},{7,12},{8,3},{9,2},... | collective-permute-start | bytes 396296 | tf_op jit(solution)/shard_map/ppermute | solution.py:344
  59.0 16.4 %collective-permute-start.8 = (f32[258,1,128]{2,1,0:T(1,128)}, f32[258,1,128]{2,1,0:T(1,128)S(1)}, u32[]{:S(2)}, u32[]{:S(2)}) collective-permute-start(f32[258,1,128]{2,1,0:T(1,128)} %get-tuple-element.58), channel_id=1, source_target_pairs={{0,12},{1,13},{2,14},{3,15},{4,8},{5,9},{6,10},{7,11},{8,4},{9,5},... | collective-permute-start | bytes 396296 | tf_op jit(solution)/shard_map/ppermute | solution.py:344
  63.5 15.9 %collective-permute-start.9 = (f32[258,1,128]{2,1,0:T(1,128)}, f32[258,1,128]{2,1,0:T(1,128)S(1)}, u32[]{:S(2)}, u32[]{:S(2)}) collective-permute-start(f32[258,1,128]{2,1,0:T(1,128)} %get-tuple-element.59), channel_id=1, source_target_pairs={{0,13},{1,12},{2,15},{3,14},{4,9},{5,8},{6,11},{7,10},{8,5},{9,4},... | collective-permute-start | bytes 396296 | tf_op jit(solution)/shard_map/ppermute | solution.py:344
  65.2 18.5 %collective-permute-start.10 = (f32[258,1,128]{2,1,0:T(1,128)}, f32[258,1,128]{2,1,0:T(1,128)S(1)}, u32[]{:S(2)}, u32[]{:S(2)}) collective-permute-start(f32[258,1,128]{2,1,0:T(1,128)} %get-tuple-element.60), channel_id=1, source_target_pairs={{0,14},{1,15},{2,12},{3,13},{4,10},{5,11},{6,8},{7,9},{8,6},{9,7},... | collective-permute-start | bytes 396296 | tf_op jit(solution)/shard_map/ppermute | solution.py:344
  65.4 18.5 %collective-permute-start.11 = (f32[258,1,128]{2,1,0:T(1,128)}, f32[258,1,128]{2,1,0:T(1,128)S(1)}, u32[]{:S(2)}, u32[]{:S(2)}) collective-permute-start(f32[258,1,128]{2,1,0:T(1,128)} %get-tuple-element.61), channel_id=1, source_target_pairs={{0,15},{1,14},{2,13},{3,12},{4,11},{5,10},{6,9},{7,8},{8,7},{9,6},... | collective-permute-start | bytes 396296 | tf_op jit(solution)/shard_map/ppermute | solution.py:344
  67.5 16.4 %collective-permute-start.12 = (f32[258,1,128]{2,1,0:T(1,128)}, f32[258,1,128]{2,1,0:T(1,128)S(1)}, u32[]{:S(2)}, u32[]{:S(2)}) collective-permute-start(f32[258,1,128]{2,1,0:T(1,128)} %get-tuple-element.62), channel_id=1, source_target_pairs={{0,16},{1,17},{2,18},{3,19},{4,20},{5,21},{6,22},{7,23},{8,24},{9,... | collective-permute-start | bytes 396296 | tf_op jit(solution)/shard_map/ppermute | solution.py:344
  75.5 29.2 %collective-permute-start.17 = (f32[516,1,128]{2,1,0:T(1,128)}, f32[516,1,128]{2,1,0:T(1,128)S(1)}, u32[]{:S(2)}, u32[]{:S(2)}) collective-permute-start(f32[516,1,128]{2,1,0:T(1,128)} %get-tuple-element.71), channel_id=1, source_target_pairs={{0,2},{1,3},{2,0},{3,1},{4,6},{5,7},{6,4},{7,5},{8,10},{9,11},{10,... | collective-permute-start | bytes 792584 | tf_op jit(solution)/shard_map/ppermute | solution.py:344
  79.4 26.6 %collective-permute-start.18 = (f32[516,1,128]{2,1,0:T(1,128)}, f32[516,1,128]{2,1,0:T(1,128)S(1)}, u32[]{:S(2)}, u32[]{:S(2)}) collective-permute-start(f32[516,1,128]{2,1,0:T(1,128)} %get-tuple-element.72), channel_id=1, source_target_pairs={{0,24},{1,25},{2,26},{3,27},{4,28},{5,29},{6,30},{7,31},{8,16},{9,... | collective-permute-start | bytes 792584 | tf_op jit(solution)/shard_map/ppermute | solution.py:344
  83.7 15.3 %collective-permute-start.13 = (f32[258,1,128]{2,1,0:T(1,128)}, f32[258,1,128]{2,1,0:T(1,128)S(1)}, u32[]{:S(2)}, u32[]{:S(2)}) collective-permute-start(f32[258,1,128]{2,1,0:T(1,128)} %get-tuple-element.63), channel_id=1, source_target_pairs={{0,17},{1,16},{2,19},{3,18},{4,21},{5,20},{6,23},{7,22},{8,25},{9,... | collective-permute-start | bytes 396296 | tf_op jit(solution)/shard_map/ppermute | solution.py:344
  83.9 15.1 %collective-permute-start.14 = (f32[258,1,128]{2,1,0:T(1,128)}, f32[258,1,128]{2,1,0:T(1,128)S(1)}, u32[]{:S(2)}, u32[]{:S(2)}) collective-permute-start(f32[258,1,128]{2,1,0:T(1,128)} %get-tuple-element.64), channel_id=1, source_target_pairs={{0,18},{1,19},{2,16},{3,17},{4,22},{5,23},{6,20},{7,21},{8,26},{9,... | collective-permute-start | bytes 396296 | tf_op jit(solution)/shard_map/ppermute | solution.py:344
  83.9 18.9 %collective-permute-start.15 = (f32[258,1,128]{2,1,0:T(1,128)}, f32[258,1,128]{2,1,0:T(1,128)S(1)}, u32[]{:S(2)}, u32[]{:S(2)}) collective-permute-start(f32[258,1,128]{2,1,0:T(1,128)} %get-tuple-element.65), channel_id=1, source_target_pairs={{0,19},{1,18},{2,17},{3,16},{4,23},{5,22},{6,21},{7,20},{8,27},{9,... | collective-permute-start | bytes 396296 | tf_op jit(solution)/shard_map/ppermute | solution.py:344
  98.9 11.2 %collective-permute-start.19 = (f32[516,1,128]{2,1,0:T(1,128)}, f32[516,1,128]{2,1,0:T(1,128)S(1)}, u32[]{:S(2)}, u32[]{:S(2)}) collective-permute-start(f32[516,1,128]{2,1,0:T(1,128)} %get-tuple-element.73), channel_id=1, source_target_pairs={{0,26},{1,27},{2,24},{3,25},{4,30},{5,31},{6,28},{7,29},{8,18},{9,... | collective-permute-start | bytes 792584 | tf_op jit(solution)/shard_map/ppermute | solution.py:344
  98.9 34.2 %collective-permute-start.20 = (f32[516,1,128]{2,1,0:T(1,128)}, f32[516,1,128]{2,1,0:T(1,128)S(1)}, u32[]{:S(2)}, u32[]{:S(2)}) collective-permute-start(f32[516,1,128]{2,1,0:T(1,128)} %get-tuple-element.78), channel_id=1, source_target_pairs={{0,20},{1,21},{2,22},{3,23},{4,16},{5,17},{6,18},{7,19},{8,28},{9,... | collective-permute-start | bytes 792584 | tf_op jit(solution)/shard_map/ppermute | solution.py:344
  102.8 38.0 %collective-permute-start.21 = (f32[516,1,128]{2,1,0:T(1,128)}, f32[516,1,128]{2,1,0:T(1,128)S(1)}, u32[]{:S(2)}, u32[]{:S(2)}) collective-permute-start(f32[516,1,128]{2,1,0:T(1,128)} %get-tuple-element.79), channel_id=1, source_target_pairs={{0,22},{1,23},{2,20},{3,21},{4,18},{5,19},{6,16},{7,17},{8,30},{9,... | collective-permute-start | bytes 792584 | tf_op jit(solution)/shard_map/ppermute | solution.py:344
  104.7 53.4 %collective-permute-start.22 = (f32[516,1,128]{2,1,0:T(1,128)}, f32[516,1,128]{2,1,0:T(1,128)S(1)}, u32[]{:S(2)}, u32[]{:S(2)}) collective-permute-start(f32[516,1,128]{2,1,0:T(1,128)} %get-tuple-element.84), channel_id=1, source_target_pairs={{0,28},{1,29},{2,30},{3,31},{4,24},{5,25},{6,26},{7,27},{8,20},{9,... | collective-permute-start | bytes 792584 | tf_op jit(solution)/shard_map/ppermute | solution.py:344
  106.0 53.5 %collective-permute-start.23 = (f32[516,1,128]{2,1,0:T(1,128)}, f32[516,1,128]{2,1,0:T(1,128)S(1)}, u32[]{:S(2)}, u32[]{:S(2)}) collective-permute-start(f32[516,1,128]{2,1,0:T(1,128)} %get-tuple-element.89), channel_id=1, source_target_pairs={{0,30},{1,31},{2,28},{3,29},{4,26},{5,27},{6,24},{7,25},{8,22},{9,... | collective-permute-start | bytes 792584 | tf_op jit(solution)/shard_map/ppermute | solution.py:344
  110.2 49.3 %collective-permute-start.34 = (f32[64,128]{1,0:T(8,128)S(1)}, f32[64,128]{1,0:T(8,128)S(1)}, u32[]{:S(2)}, u32[]{:S(2)}) collective-permute-start(f32[64,128]{1,0:T(8,128)S(1)} %shard_map.74.refs_6_), channel_id=1, source_target_pairs={{0,24},{8,16},{16,8},{24,0},{1,25},{9,17},{17,9},{25,1},{2,26},{10... | collective-permute-start | bytes 98312 | tf_op jit(solution)/shard_map/ppermute | solution.py:344
  133.1 26.4 %collective-permute-start.33 = (f32[64,128]{1,0:T(8,128)S(1)}, f32[64,128]{1,0:T(8,128)S(1)}, u32[]{:S(2)}, u32[]{:S(2)}) collective-permute-start(f32[64,128]{1,0:T(8,128)S(1)} %shard_map.74.refs_6_), channel_id=1, source_target_pairs={{0,16},{8,24},{16,0},{24,8},{1,17},{9,25},{17,1},{25,9},{2,18},{10... | collective-permute-start | bytes 98312 | tf_op jit(solution)/shard_map/ppermute | solution.py:344
  140.8 18.8 %collective-permute-start.32 = (f32[64,128]{1,0:T(8,128)S(1)}, f32[64,128]{1,0:T(8,128)S(1)}, u32[]{:S(2)}, u32[]{:S(2)}) collective-permute-start(f32[64,128]{1,0:T(8,128)S(1)} %shard_map.74.refs_6_), channel_id=1, source_target_pairs={{0,8},{8,0},{16,24},{24,16},{1,9},{9,1},{17,25},{25,17},{2,10},{10... | collective-permute-start | bytes 98312 | tf_op jit(solution)/shard_map/ppermute | solution.py:344
  141.6 1.0 copy-start.1
  158.1 1.5 copy-start.2
where the time goes:
time: 165 us
  waiting for transfers between devices  74.5 us (45%)
  starting transfers between devices  44.8 us (27%)
  Pallas kernels  43.4 us (26%)
    ppermute x35, waiting for transfers between devices, swap(): return lax.ppermute(x, axis, [(s, s ^ k) for s in range(size)])  74.5 us
    ppermute x35, starting transfers between devices, swap(): return lax.ppermute(x, axis, [(s, s ^ k) for s in range(size)])  44.8 us
    pallas_call x5, Pallas kernels, apply_blocks(): pl.pallas_call(functools.partial(apply_kernel, slots, len(blocks), len(ho...  22 us
    pallas_call x3, Pallas kernels, pack(): pl.pallas_call(functools.partial(pack_kernel, n, slots, messages, passed...  17.3 us
    pallas_call x1, Pallas kernels, plan(): pl.pallas_call(functools.partial(plan_kernel, n, n_dev, slots, rows_dev,...  4.14 us
  transfers between devices with their start and end apart: 35, of which 16 were waited for; matrix products, arithmetic and copies ran while one was open for 0% of the time, Pallas kernels for 17%

commit v1 on v0

--- a/solution.py
+++ b/solution.py
@@ -38,7 +38,6 @@
     load_row.start()
     load.start()
     load_owner.wait()
-    load_row.wait()
     me = lax.axis_index("grp") * n_dev + lax.axis_index("dev")
     blocks = owner_ref.shape[0]
     id_rows = id_rows_of(slots)
@@ -55,6 +54,7 @@
         onehot_ref[r * n : (r + 1) * n, :] = hit.astype(jnp.float32).astype(jnp.bfloat16)
     inclusive = jnp.dot(onehot_ref[...], upper, preferred_element_type=jnp.float32)
     base = jnp.full((n, 1), -1.0, jnp.float32)
+    load_row.wait()
     row1 = row_vmem[...] + 1
     for r in range(blocks):
         hit = owner_at == partner[r : r + 1, :]
@@ -76,9 +76,15 @@
     for q in range(id_rows):
         index_out[q * n : (q + 1) * n, :] = index[:, q * LANES : (q + 1) * LANES]
         ids_out[q * n : (q + 1) * n, :] = ids[:, q * LANES : (q + 1) * LANES]
-    to_smem = pltpu.make_async_copy(index_out, index_smem, sem2)
-    to_smem.start()
-    to_smem.wait()
+    low = min(ks) // 8 * 8
+    count = -(-(max(ks) + 1 - low) // 8) * 8
+    moves = []
+    for q in range(id_rows):
+        rows = pl.ds(q * n + low, count)
+        moves.append(pltpu.make_async_copy(index_out.at[rows], index_smem.at[rows], sem2))
+        moves[q].start()
+    for move in moves:
+        move.wait()
     load.wait()
     for k, out in zip(ks, outs):
         for j in range(slots):
@@ -376,7 +382,7 @@
     hot = hot_ids.shape[0]
     slots = max(4, 2 * cold_grads.shape[0] // n)
     near, cross = partner_order(n, n_dev)
-    first, second = cores_of(cross[0]), cores_of(near[1] + cross[1] + near[2])
+    first, second = cores_of(cross[0]), cores_of(near[1] + near[2] + cross[1])
     rest = cross[2] + near[0] + near[3] + cross[3] + [0]
     index, ids, *blocks = plan(n, n_dev, slots, rows_dev, first, cold_owner[:, 0], cold_row, cold_grads)
     blocks += pack(n, slots, [[("own", k)] for k in second], index, ids, cold_grads)

time: 165 us -> 157 us (0.952)
  the two profiles are of different devices: /device:TPU:8 before, /device:TPU:20 now
where the time goes in v1:
time: 157 us; the launch traced here: 156 us
  waiting for transfers between devices  70.8 us (45%)
  Pallas kernels  43.5 us (28%)
  starting transfers between devices  40.2 us (26%)
    ppermute x35, waiting for transfers between devices, swap(): return lax.ppermute(x, axis, [(s, s ^ k) for s in range(size)])  70.8 us
    ppermute x35, starting transfers between devices, swap(): return lax.ppermute(x, axis, [(s, s ^ k) for s in range(size)])  40.2 us
    pallas_call x5, Pallas kernels, apply_blocks(): pl.pallas_call(functools.partial(apply_kernel, slots, len(blocks), len(ho...  22.4 us
    pallas_call x3, Pallas kernels, pack(): pl.pallas_call(functools.partial(pack_kernel, n, slots, messages, passed...  17.3 us
    pallas_call x1, Pallas kernels, plan(): pl.pallas_call(functools.partial(plan_kernel, n, n_dev, slots, rows_dev,...  3.8 us
  transfers between devices with their start and end apart: 35, of which 14 were waited for; matrix products, arithmetic and copies ran while one was open for 0% of the time, Pallas kernels for 19%

profile of v1, /device:TPU:20, one launch (start us, length us, event | category | flops | bytes accessed | tf_op | source)
XLA Modules:
  0.0 156.5 jit_solution(15718814859021082626)
XLA Ops:
  0.0 3.8 %plan.1 = (s32[64,128]{1,0:T(8,128)S(1)}, f32[64,128]{1,0:T(8,128)S(1)}, f32[258,1,128]{2,1,0:T(1,128)S(1)}, f32[258,1,128]{2,1,0:T(1,128)S(1)}, f32[258,1,128]{2,1,0:T(1,128)S(1)}, /*index=5*/f32[258,1,128]{2,1,0:T(1,128)S(1)}) custom-call(s32[32,128]{1,0:T(8,128)} %bitcast.7, s32[32,128]{1,0:T(8,128)} %bitcast.8, f32[4096,128]{1,0:T(8,128)} %grads_ref.7), custom_call_target="tpu_custom_call" | custom-call | tf_op jit(solution)/shard_map/plan/pallas_call | solution.py:151
  3.8 5.5 %pack.4 = f32[2064,1,128]{2,1,0:T(1,128)} custom-call(s32[8192]{0:T(1024)S(1)} %bitcast.4, f32[64,128]{1,0:T(8,128)S(1)} %get-tuple-element.53.ids_ref, f32[4096,128]{1,0:T(8,128)} %grads_ref.7), custom_call_target="tpu_custom_call" | custom-call | tf_op jit(solution)/shard_map/pack/pallas_call | solution.py:179
  9.4 0.1 collective-permute-start.16
  9.5 0.7 fusion
  10.2 1.6 collective-permute-start.24
  11.8 0.5 collective-permute-start.26
  12.2 1.5 collective-permute-start.25
  13.8 0.4 collective-permute-done.24
  14.2 2.4 %collective-permute-done.26 = f32[64,128]{1,0:T(8,128)S(1)} collective-permute-done((f32[64,128]{1,0:T(8,128)S(1)}, f32[64,128]{1,0:T(8,128)S(1)}, u32[]{:S(2)}, u32[]{:S(2)}) %collective-permute-start.26) | collective-permute-done | bytes 32800 | tf_op jit(solution)/shard_map/ppermute | solution.py:350
  16.6 0.0 collective-permute-done.25
  16.6 0.1 collective-permute-start.27
  16.7 0.4 collective-permute-start
  17.1 2.3 %collective-permute-start.1 = (f32[258,1,128]{2,1,0:T(1,128)S(1)}, f32[258,1,128]{2,1,0:T(1,128)S(1)}, u32[]{:S(2)}, u32[]{:S(2)}) collective-permute-start(f32[258,1,128]{2,1,0:T(1,128)S(1)} %get-tuple-element.49), channel_id=1, source_target_pairs={{0,5},{1,4},{2,7},{3,6},{4,1},{5,0},{6,3},{7,2},{8,13},{9,12},{10,... | collective-permute-start | bytes 396296 | tf_op jit(solution)/shard_map/ppermute | solution.py:350
  19.4 0.0 collective-permute-done.27
  19.4 0.5 collective-permute-start.30
  20.0 3.5 %collective-permute-start.29 = (f32[32,128]{1,0:T(8,128)S(1)}, f32[32,128]{1,0:T(8,128)S(1)}, u32[]{:S(2)}, u32[]{:S(2)}) collective-permute-start(f32[32,128]{1,0:T(8,128)S(1)} %dynamic-slice_add_fusion.refs_0_), channel_id=1, source_target_pairs={{0,4},{1,5},{2,6},{3,7},{4,0},{5,1},{6,2},{7,3},{8,12},{9,13},{10,... | collective-permute-start | bytes 49160 | tf_op jit(solution)/shard_map/ppermute | solution.py:350
  23.4 9.7 %collective-permute-done.30.refs_3_ = f32[32,128]{1,0:T(8,128)S(1)} collective-permute-done((f32[32,128]{1,0:T(8,128)S(1)}, f32[32,128]{1,0:T(8,128)S(1)}, u32[]{:S(2)}, u32[]{:S(2)}) %collective-permute-start.30) | collective-permute-done | bytes 16416 | tf_op jit(solution)/shard_map/ppermute | solution.py:350
  33.1 0.0 collective-permute-done.29.refs_2_
  33.1 3.7 %collective-permute-done.28.refs_1_ = f32[32,128]{1,0:T(8,128)S(1)} collective-permute-done((f32[32,128]{1,0:T(8,128)S(1)}, f32[32,128]{1,0:T(8,128)S(1)}, u32[]{:S(2)}, u32[]{:S(2)}) %collective-permute-start.28) | collective-permute-done | bytes 16416 | tf_op jit(solution)/shard_map/ppermute | solution.py:350
  36.9 0.1 collective-permute-start.2
  36.9 1.1 collective-permute-done.31.b_ref
  38.0 0.7 collective-permute-start.3
  38.7 6.4 %pack.3 = (f32[258,1,128]{2,1,0:T(1,128)}, f32[258,1,128]{2,1,0:T(1,128)}, f32[258,1,128]{2,1,0:T(1,128)}, f32[258,1,128]{2,1,0:T(1,128)}, f32[258,1,128]{2,1,0:...) custom-call(s32[8192]{0:T(1024)S(1)} %bitcast.5, ...), custom_call_target="tpu_custom_call" | custom-call | tf_op jit(solution)/shard_map/pack/pallas_call | solution.py:179
  45.1 1.1 collective-permute-start.4
  46.2 0.0 collective-permute-done.1.refs_2_
  46.2 0.6 collective-permute-start.5
  46.9 2.0 %collective-permute-done.2.refs_3_ = f32[258,1,128]{2,1,0:T(1,128)S(1)} collective-permute-done((f32[258,1,128]{2,1,0:T(1,128)S(1)}, f32[258,1,128]{2,1,0:T(1,128)S(1)}, u32[]{:S(2)}, u32[]{:S(2)}) %collective-permute-start.2) | collective-permute-done | bytes 132128 | tf_op jit(solution)/shard_map/ppermute | solution.py:350
  48.9 0.3 collective-permute-start.6
  49.2 1.6 %collective-permute-done.3.refs_4_ = f32[258,1,128]{2,1,0:T(1,128)S(1)} collective-permute-done((f32[258,1,128]{2,1,0:T(1,128)S(1)}, f32[258,1,128]{2,1,0:T(1,128)S(1)}, u32[]{:S(2)}, u32[]{:S(2)}) %collective-permute-start.3) | collective-permute-done | bytes 132128 | tf_op jit(solution)/shard_map/ppermute | solution.py:350
  50.8 0.0 collective-permute-start.7
  50.8 0.9 collective-permute-done.4.refs_5_
  51.8 1.1 collective-permute-start.8
  52.9 6.2 %collective-permute-done.5.refs_6_ = f32[258,1,128]{2,1,0:T(1,128)S(1)} collective-permute-done((f32[258,1,128]{2,1,0:T(1,128)}, f32[258,1,128]{2,1,0:T(1,128)S(1)}, u32[]{:S(2)}, u32[]{:S(2)}) %collective-permute-start.5) | collective-permute-done | bytes 132128 | tf_op jit(solution)/shard_map/ppermute | solution.py:350
  59.0 1.1 collective-permute-start.9
  60.2 2.2 %collective-permute-start.10 = (f32[258,1,128]{2,1,0:T(1,128)}, f32[258,1,128]{2,1,0:T(1,128)S(1)}, u32[]{:S(2)}, u32[]{:S(2)}) collective-permute-start(f32[258,1,128]{2,1,0:T(1,128)} %get-tuple-element.60), channel_id=1, source_target_pairs={{0,18},{1,19},{2,16},{3,17},{4,22},{5,23},{6,20},{7,21},{8,26},{9,... | collective-permute-start | bytes 396296 | tf_op jit(solution)/shard_map/ppermute | solution.py:350
  62.3 0.2 collective-permute-start.11
  62.5 0.0 collective-permute-done.16.refs_0_
  62.5 2.4 %collective-permute-start.12 = (f32[258,1,128]{2,1,0:T(1,128)}, f32[258,1,128]{2,1,0:T(1,128)S(1)}, u32[]{:S(2)}, u32[]{:S(2)}) collective-permute-start(f32[258,1,128]{2,1,0:T(1,128)} %get-tuple-element.62), channel_id=1, source_target_pairs={{0,12},{1,13},{2,14},{3,15},{4,8},{5,9},{6,10},{7,11},{8,4},{9,5},... | collective-permute-start | bytes 396296 | tf_op jit(solution)/shard_map/ppermute | solution.py:350
  64.9 5.4 %pack.5 = (f32[516,1,128]{2,1,0:T(1,128)}, f32[516,1,128]{2,1,0:T(1,128)}, f32[516,1,128]{2,1,0:T(1,128)}, f32[516,1,128]{2,1,0:T(1,128)}, f32[516,1,128]{2,1,0:...) custom-call(s32[8192]{0:T(1024)S(1)} %bitcast.6, ...), custom_call_target="tpu_custom_call" | custom-call | tf_op jit(solution)/shard_map/pack/pallas_call | solution.py:179
  70.3 0.0 collective-permute-done.8.refs_9_
  70.3 1.2 collective-permute-start.17
  71.5 0.9 collective-permute-start.18
  72.4 2.2 %collective-permute-start.13 = (f32[258,1,128]{2,1,0:T(1,128)}, f32[258,1,128]{2,1,0:T(1,128)S(1)}, u32[]{:S(2)}, u32[]{:S(2)}) collective-permute-start(f32[258,1,128]{2,1,0:T(1,128)} %get-tuple-element.63), channel_id=1, source_target_pairs={{0,13},{1,12},{2,15},{3,14},{4,9},{5,8},{6,11},{7,10},{8,5},{9,4},... | collective-permute-start | bytes 396296 | tf_op jit(solution)/shard_map/ppermute | solution.py:350
  74.6 0.0 collective-permute-done.11.refs_12_
  74.6 1.1 collective-permute-start.14
  75.7 1.7 %collective-permute-start.15 = (f32[258,1,128]{2,1,0:T(1,128)}, f32[258,1,128]{2,1,0:T(1,128)S(1)}, u32[]{:S(2)}, u32[]{:S(2)}) collective-permute-start(f32[258,1,128]{2,1,0:T(1,128)} %get-tuple-element.65), channel_id=1, source_target_pairs={{0,15},{1,14},{2,13},{3,12},{4,11},{5,10},{6,9},{7,8},{8,7},{9,6},... | collective-permute-start | bytes 396296 | tf_op jit(solution)/shard_map/ppermute | solution.py:350
  77.4 9.8 %collective-permute-done.13.refs_14_ = f32[258,1,128]{2,1,0:T(1,128)S(1)} collective-permute-done((f32[258,1,128]{2,1,0:T(1,128)}, f32[258,1,128]{2,1,0:T(1,128)S(1)}, u32[]{:S(2)}, u32[]{:S(2)}) %collective-permute-start.13) | collective-permute-done | bytes 132128 | tf_op jit(solution)/shard_map/ppermute | solution.py:350
  87.3 4.3 %collective-permute-done.14.refs_15_ = f32[258,1,128]{2,1,0:T(1,128)S(1)} collective-permute-done((f32[258,1,128]{2,1,0:T(1,128)}, f32[258,1,128]{2,1,0:T(1,128)S(1)}, u32[]{:S(2)}, u32[]{:S(2)}) %collective-permute-start.14) | collective-permute-done | bytes 132128 | tf_op jit(solution)/shard_map/ppermute | solution.py:350
  91.6 3.0 %collective-permute-done.15.refs_16_ = f32[258,1,128]{2,1,0:T(1,128)S(1)} collective-permute-done((f32[258,1,128]{2,1,0:T(1,128)}, f32[258,1,128]{2,1,0:T(1,128)S(1)}, u32[]{:S(2)}, u32[]{:S(2)}) %collective-permute-start.15) | collective-permute-done | bytes 132128 | tf_op jit(solution)/shard_map/ppermute | solution.py:350
  94.6 3.7 %collective-permute-start.21 = (f32[516,1,128]{2,1,0:T(1,128)}, f32[516,1,128]{2,1,0:T(1,128)S(1)}, u32[]{:S(2)}, u32[]{:S(2)}) collective-permute-start(f32[516,1,128]{2,1,0:T(1,128)} %get-tuple-element.79), channel_id=1, source_target_pairs={{0,22},{1,23},{2,20},{3,21},{4,18},{5,19},{6,16},{7,17},{8,30},{9,... | collective-permute-start | bytes 792584 | tf_op jit(solution)/shard_map/ppermute | solution.py:350
  98.3 1.1 collective-permute-start.22
  99.4 0.8 collective-permute-start.23
  100.2 3.3 %collective-permute-start.34 = (f32[64,128]{1,0:T(8,128)S(1)}, f32[64,128]{1,0:T(8,128)S(1)}, u32[]{:S(2)}, u32[]{:S(2)}) collective-permute-start(f32[64,128]{1,0:T(8,128)S(1)} %shard_map.74.refs_6_), channel_id=1, source_target_pairs={{0,24},{8,16},{16,8},{24,0},{1,25},{9,17},{17,9},{25,1},{2,26},{10... | collective-permute-start | bytes 98312 | tf_op jit(solution)/shard_map/ppermute | solution.py:350
  103.5 20.0 %collective-permute-done.20.refs_4_ = f32[516,1,128]{2,1,0:T(1,128)S(1)} collective-permute-done((f32[516,1,128]{2,1,0:T(1,128)}, f32[516,1,128]{2,1,0:T(1,128)S(1)}, u32[]{:S(2)}, u32[]{:S(2)}) %collective-permute-start.20) | collective-permute-done | bytes 264224 | tf_op jit(solution)/shard_map/ppermute | solution.py:350
  123.4 1.6 %collective-permute-start.33 = (f32[64,128]{1,0:T(8,128)S(1)}, f32[64,128]{1,0:T(8,128)S(1)}, u32[]{:S(2)}, u32[]{:S(2)}) collective-permute-start(f32[64,128]{1,0:T(8,128)S(1)} %shard_map.74.refs_6_), channel_id=1, source_target_pairs={{0,16},{8,24},{16,0},{24,8},{1,17},{9,25},{17,1},{25,9},{2,18},{10... | collective-permute-start | bytes 98312 | tf_op jit(solution)/shard_map/ppermute | solution.py:350
  125.0 5.6 %collective-permute-done.21.refs_5_ = f32[516,1,128]{2,1,0:T(1,128)S(1)} collective-permute-done((f32[516,1,128]{2,1,0:T(1,128)}, f32[516,1,128]{2,1,0:T(1,128)S(1)}, u32[]{:S(2)}, u32[]{:S(2)}) %collective-permute-start.21) | collective-permute-done | bytes 264224 | tf_op jit(solution)/shard_map/ppermute | solution.py:350
  130.6 2.4 %collective-permute-start.32 = (f32[64,128]{1,0:T(8,128)S(1)}, f32[64,128]{1,0:T(8,128)S(1)}, u32[]{:S(2)}, u32[]{:S(2)}) collective-permute-start(f32[64,128]{1,0:T(8,128)S(1)} %shard_map.74.refs_6_), channel_id=1, source_target_pairs={{0,8},{8,0},{16,24},{24,16},{1,9},{9,1},{17,25},{25,17},{2,10},{10... | collective-permute-start | bytes 98312 | tf_op jit(solution)/shard_map/ppermute | solution.py:350
  133.0 0.9 copy-done.1
  134.0 10.2 %apply.5 = (f32[8200,128]{1,0:T(8,128)S(1)}, f32[8200,128]{1,0:T(8,128)S(1)}, f32[8200,128]{1,0:T(8,128)S(1)}, f32[8200,128]{1,0:T(8,128)S(1)}) custom-call(f32[8192,128]{1,0:T(8,128)} %refs_0_.1, f32[258,1,128]{2,1,0:T(1,128)S(1)} %collective-permute-done.refs_1_, f32[258,1,128]{2,1,0:T(1,128)S(1)} %collective-permute-done.1.refs_2_, ...), custom_call_target="tpu_custom_call" | custom-call | tf_op jit(solution)/shard_map/apply/pallas_call | solution.py:303
  144.2 3.2 %apply.6 = (f32[8200,128]{1,0:T(8,128)S(1)}, f32[8200,128]{1,0:T(8,128)S(1)}, f32[8200,128]{1,0:T(8,128)S(1)}, f32[8200,128]{1,0:T(8,128)S(1)}) custom-call(f32[8200,128]{1,0:T(8,128)S(1)} %get-tuple-element.67.refs_0_, f32[8200,128]{1,0:T(8,128)S(1)} %get-tuple-element.68.refs_1_, ...), custom_call_target="tpu_custom_call", output_to_operand_aliasing={{0}: (0, {}), {1}: (1, {}), {2}: (2, {}), {3}: (3, {})} | custom-call | tf_op jit(solution)/shard_map/apply/pallas_call | solution.py:303
  147.4 2.4 %apply.7 = (f32[8200,128]{1,0:T(8,128)S(1)}, f32[8200,128]{1,0:T(8,128)S(1)}, f32[8200,128]{1,0:T(8,128)S(1)}, f32[8200,128]{1,0:T(8,128)S(1)}) custom-call(f32[8200,128]{1,0:T(8,128)S(1)} %get-tuple-element.74.refs_0_, f32[8200,128]{1,0:T(8,128)S(1)} %get-tuple-element.75.refs_1_, ...), custom_call_target="tpu_custom_call", output_to_operand_aliasing={{0}: (0, {}), {1}: (1, {}), {2}: (2, {}), {3}: (3, {})} | custom-call | tf_op jit(solution)/shard_map/apply/pallas_call | solution.py:303
  149.8 0.0 copy-start.2
  149.8 1.5 apply.8
  151.4 5.1 %apply.9 = (f32[8200,128]{1,0:T(8,128)S(1)}, f32[8200,128]{1,0:T(8,128)S(1)}, f32[8200,128]{1,0:T(8,128)S(1)}, f32[8200,128]{1,0:T(8,128)S(1)}, f32[8192,128]{1,0:T(8,128)}) custom-call(f32[8200,128]{1,0:T(8,128)S(1)} %get-tuple-element.85.refs_0_, ...), custom_call_target="tpu_custom_call", output_to_operand_aliasing={{0}: (0, {}), {1}: (1, {}), {2}: (2, {}), {3}: (3, {})} | custom-call | tf_op jit(solution)/shard_map/apply/pallas_call | solution.py:303
  (30 shorter events, 0.1 us)
Async XLA Ops:
  0.0 9.4 %copy-start = (f32[1024,128]{1,0:T(8,128)S(1)}, f32[1024,128]{1,0:T(8,128)}, u32[]{:S(2)}) copy-start(f32[1024,128]{1,0:T(8,128)} %param.11) | copy-start | bytes 1572868
  0.0 9.5 %copy-start.3 = (s32[1024]{0:T(1024)S(1)}, s32[1024]{0:T(1024)}, u32[]{:S(2)}) copy-start(s32[1024]{0:T(1024)} %param.12) | copy-start | bytes 12292
  9.4 53.1 %collective-permute-start.16 = (f32[2064,1,128]{2,1,0:T(1,128)}, f32[2064,1,128]{2,1,0:T(1,128)S(1)}, u32[]{:S(2)}, u32[]{:S(2)}) collective-permute-start(f32[2064,1,128]{2,1,0:T(1,128)} %pack.4), channel_id=1, source_target_pairs={{0,1},{1,0},{2,3},{3,2},{4,5},{5,4},{6,7},{7,6},{8,9},{9,8},{10,11... | collective-permute-start | bytes 3170312 | tf_op jit(solution)/shard_map/ppermute | solution.py:350
  10.2 4.0 %collective-permute-start.24 = (f32[64,128]{1,0:T(8,128)S(1)}, f32[64,128]{1,0:T(8,128)S(1)}, u32[]{:S(2)}, u32[]{:S(2)}) collective-permute-start(f32[64,128]{1,0:T(8,128)S(1)} %get-tuple-element.91), channel_id=1, source_target_pairs={{0,8},{8,0},{16,24},{24,16},{1,9},{9,1},{17,25},{25,17},{2,10},{10... | collective-permute-start | bytes 98312 | tf_op jit(solution)/shard_map/ppermute | solution.py:350
  11.8 4.8 %collective-permute-start.26 = (f32[64,128]{1,0:T(8,128)S(1)}, f32[64,128]{1,0:T(8,128)S(1)}, u32[]{:S(2)}, u32[]{:S(2)}) collective-permute-start(f32[64,128]{1,0:T(8,128)S(1)} %get-tuple-element.92), channel_id=1, source_target_pairs={{0,24},{8,16},{16,8},{24,0},{1,25},{9,17},{17,9},{25,1},{2,26},{10... | collective-permute-start | bytes 98312 | tf_op jit(solution)/shard_map/ppermute | solution.py:350
  12.2 4.3 %collective-permute-start.25 = (f32[64,128]{1,0:T(8,128)S(1)}, f32[64,128]{1,0:T(8,128)S(1)}, u32[]{:S(2)}, u32[]{:S(2)}) collective-permute-start(f32[64,128]{1,0:T(8,128)S(1)} %get-tuple-element.93), channel_id=1, source_target_pairs={{0,16},{8,24},{16,0},{24,8},{1,17},{9,25},{17,1},{25,9},{2,18},{10... | collective-permute-start | bytes 98312 | tf_op jit(solution)/shard_map/ppermute | solution.py:350
  16.6 2.8 %collective-permute-start.27 = (f32[32,128]{1,0:T(8,128)S(1)}, f32[32,128]{1,0:T(8,128)S(1)}, u32[]{:S(2)}, u32[]{:S(2)}) collective-permute-start(f32[32,128]{1,0:T(8,128)S(1)} %constant_dynamic-slice_fusion), channel_id=1, source_target_pairs={{0,1},{1,0},{2,3},{3,2},{4,5},{5,4},{6,7},{7,6},{8,9},{9,8},{10,11... | collective-permute-start | bytes 49160 | tf_op jit(solution)/shard_map/ppermute | solution.py:350
  16.7 28.4 %collective-permute-start = (f32[258,1,128]{2,1,0:T(1,128)S(1)}, f32[258,1,128]{2,1,0:T(1,128)S(1)}, u32[]{:S(2)}, u32[]{:S(2)}) collective-permute-start(f32[258,1,128]{2,1,0:T(1,128)S(1)} %get-tuple-element.48), channel_id=1, source_target_pairs={{0,4},{1,5},{2,6},{3,7},{4,0},{5,1},{6,2},{7,3},{8,12},{9,13},{10,... | collective-permute-start | bytes 396296 | tf_op jit(solution)/shard_map/ppermute | solution.py:350
  17.1 29.1 %collective-permute-start.1 = (f32[258,1,128]{2,1,0:T(1,128)S(1)}, f32[258,1,128]{2,1,0:T(1,128)S(1)}, u32[]{:S(2)}, u32[]{:S(2)}) collective-permute-start(f32[258,1,128]{2,1,0:T(1,128)S(1)} %get-tuple-element.49), channel_id=1, source_target_pairs={{0,5},{1,4},{2,7},{3,6},{4,1},{5,0},{6,3},{7,2},{8,13},{9,12},{10,... | collective-permute-start | bytes 396296 | tf_op jit(solution)/shard_map/ppermute | solution.py:350
  19.4 13.7 %collective-permute-start.30 = (f32[32,128]{1,0:T(8,128)S(1)}, f32[32,128]{1,0:T(8,128)S(1)}, u32[]{:S(2)}, u32[]{:S(2)}) collective-permute-start(f32[32,128]{1,0:T(8,128)S(1)} %dynamic-slice_add_fusion.refs_0_), channel_id=1, source_target_pairs={{0,6},{1,7},{2,4},{3,5},{4,2},{5,3},{6,0},{7,1},{8,14},{9,15},{10,... | collective-permute-start | bytes 49160 | tf_op jit(solution)/shard_map/ppermute | solution.py:350
  20.0 13.2 %collective-permute-start.29 = (f32[32,128]{1,0:T(8,128)S(1)}, f32[32,128]{1,0:T(8,128)S(1)}, u32[]{:S(2)}, u32[]{:S(2)}) collective-permute-start(f32[32,128]{1,0:T(8,128)S(1)} %dynamic-slice_add_fusion.refs_0_), channel_id=1, source_target_pairs={{0,4},{1,5},{2,6},{3,7},{4,0},{5,1},{6,2},{7,3},{8,12},{9,13},{10,... | collective-permute-start | bytes 49160 | tf_op jit(solution)/shard_map/ppermute | solution.py:350
  33.1 3.7 %collective-permute-start.28 = (f32[32,128]{1,0:T(8,128)S(1)}, f32[32,128]{1,0:T(8,128)S(1)}, u32[]{:S(2)}, u32[]{:S(2)}) collective-permute-start(f32[32,128]{1,0:T(8,128)S(1)} %dynamic-slice_add_fusion.refs_0_), channel_id=1, source_target_pairs={{0,2},{1,3},{2,0},{3,1},{4,6},{5,7},{6,4},{7,5},{8,10},{9,11},{10,... | collective-permute-start | bytes 49160 | tf_op jit(solution)/shard_map/ppermute | solution.py:350
  36.8 1.2 collective-permute-start.31
  36.9 12.0 %collective-permute-start.2 = (f32[258,1,128]{2,1,0:T(1,128)S(1)}, f32[258,1,128]{2,1,0:T(1,128)S(1)}, u32[]{:S(2)}, u32[]{:S(2)}) collective-permute-start(f32[258,1,128]{2,1,0:T(1,128)S(1)} %get-tuple-element.50), channel_id=1, source_target_pairs={{0,6},{1,7},{2,4},{3,5},{4,2},{5,3},{6,0},{7,1},{8,14},{9,15},{10,... | collective-permute-start | bytes 396296 | tf_op jit(solution)/shard_map/ppermute | solution.py:350
  38.0 12.8 %collective-permute-start.3 = (f32[258,1,128]{2,1,0:T(1,128)S(1)}, f32[258,1,128]{2,1,0:T(1,128)S(1)}, u32[]{:S(2)}, u32[]{:S(2)}) collective-permute-start(f32[258,1,128]{2,1,0:T(1,128)S(1)} %get-tuple-element.51), channel_id=1, source_target_pairs={{0,7},{1,6},{2,5},{3,4},{4,3},{5,2},{6,1},{7,0},{8,15},{9,14},{10,... | collective-permute-start | bytes 396296 | tf_op jit(solution)/shard_map/ppermute | solution.py:350
  45.1 6.7 %collective-permute-start.4 = (f32[258,1,128]{2,1,0:T(1,128)}, f32[258,1,128]{2,1,0:T(1,128)S(1)}, u32[]{:S(2)}, u32[]{:S(2)}) collective-permute-start(f32[258,1,128]{2,1,0:T(1,128)} %get-tuple-element.54), channel_id=1, source_target_pairs={{0,8},{1,9},{2,10},{3,11},{4,12},{5,13},{6,14},{7,15},{8,0},{9,1},... | collective-permute-start | bytes 396296 | tf_op jit(solution)/shard_map/ppermute | solution.py:350
  46.2 12.8 %collective-permute-start.5 = (f32[258,1,128]{2,1,0:T(1,128)}, f32[258,1,128]{2,1,0:T(1,128)S(1)}, u32[]{:S(2)}, u32[]{:S(2)}) collective-permute-start(f32[258,1,128]{2,1,0:T(1,128)} %get-tuple-element.55), channel_id=1, source_target_pairs={{0,9},{1,8},{2,11},{3,10},{4,13},{5,12},{6,15},{7,14},{8,1},{9,0},... | collective-permute-start | bytes 396296 | tf_op jit(solution)/shard_map/ppermute | solution.py:350
  48.9 11.3 %collective-permute-start.6 = (f32[258,1,128]{2,1,0:T(1,128)}, f32[258,1,128]{2,1,0:T(1,128)S(1)}, u32[]{:S(2)}, u32[]{:S(2)}) collective-permute-start(f32[258,1,128]{2,1,0:T(1,128)} %get-tuple-element.56), channel_id=1, source_target_pairs={{0,10},{1,11},{2,8},{3,9},{4,14},{5,15},{6,12},{7,13},{8,2},{9,3},... | collective-permute-start | bytes 396296 | tf_op jit(solution)/shard_map/ppermute | solution.py:350
  50.8 11.5 %collective-permute-start.7 = (f32[258,1,128]{2,1,0:T(1,128)}, f32[258,1,128]{2,1,0:T(1,128)S(1)}, u32[]{:S(2)}, u32[]{:S(2)}) collective-permute-start(f32[258,1,128]{2,1,0:T(1,128)} %get-tuple-element.57), channel_id=1, source_target_pairs={{0,11},{1,10},{2,9},{3,8},{4,15},{5,14},{6,13},{7,12},{8,3},{9,2},... | collective-permute-start | bytes 396296 | tf_op jit(solution)/shard_map/ppermute | solution.py:350
  51.8 18.5 %collective-permute-start.8 = (f32[258,1,128]{2,1,0:T(1,128)}, f32[258,1,128]{2,1,0:T(1,128)S(1)}, u32[]{:S(2)}, u32[]{:S(2)}) collective-permute-start(f32[258,1,128]{2,1,0:T(1,128)} %get-tuple-element.58), channel_id=1, source_target_pairs={{0,16},{1,17},{2,18},{3,19},{4,20},{5,21},{6,22},{7,23},{8,24},{9,... | collective-permute-start | bytes 396296 | tf_op jit(solution)/shard_map/ppermute | solution.py:350
  59.0 12.5 %collective-permute-start.9 = (f32[258,1,128]{2,1,0:T(1,128)}, f32[258,1,128]{2,1,0:T(1,128)S(1)}, u32[]{:S(2)}, u32[]{:S(2)}) collective-permute-start(f32[258,1,128]{2,1,0:T(1,128)} %get-tuple-element.59), channel_id=1, source_target_pairs={{0,17},{1,16},{2,19},{3,18},{4,21},{5,20},{6,23},{7,22},{8,25},{9,... | collective-permute-start | bytes 396296 | tf_op jit(solution)/shard_map/ppermute | solution.py:350
  60.2 12.2 %collective-permute-start.10 = (f32[258,1,128]{2,1,0:T(1,128)}, f32[258,1,128]{2,1,0:T(1,128)S(1)}, u32[]{:S(2)}, u32[]{:S(2)}) collective-permute-start(f32[258,1,128]{2,1,0:T(1,128)} %get-tuple-element.60), channel_id=1, source_target_pairs={{0,18},{1,19},{2,16},{3,17},{4,22},{5,23},{6,20},{7,21},{8,26},{9,... | collective-permute-start | bytes 396296 | tf_op jit(solution)/shard_map/ppermute | solution.py:350
  62.3 12.2 %collective-permute-start.11 = (f32[258,1,128]{2,1,0:T(1,128)}, f32[258,1,128]{2,1,0:T(1,128)S(1)}, u32[]{:S(2)}, u32[]{:S(2)}) collective-permute-start(f32[258,1,128]{2,1,0:T(1,128)} %get-tuple-element.61), channel_id=1, source_target_pairs={{0,19},{1,18},{2,17},{3,16},{4,23},{5,22},{6,21},{7,20},{8,27},{9,... | collective-permute-start | bytes 396296 | tf_op jit(solution)/shard_map/ppermute | solution.py:350
  62.5 13.2 %collective-permute-start.12 = (f32[258,1,128]{2,1,0:T(1,128)}, f32[258,1,128]{2,1,0:T(1,128)S(1)}, u32[]{:S(2)}, u32[]{:S(2)}) collective-permute-start(f32[258,1,128]{2,1,0:T(1,128)} %get-tuple-element.62), channel_id=1, source_target_pairs={{0,12},{1,13},{2,14},{3,15},{4,8},{5,9},{6,10},{7,11},{8,4},{9,5},... | collective-permute-start | bytes 396296 | tf_op jit(solution)/shard_map/ppermute | solution.py:350
  70.3 28.0 %collective-permute-start.17 = (f32[516,1,128]{2,1,0:T(1,128)}, f32[516,1,128]{2,1,0:T(1,128)S(1)}, u32[]{:S(2)}, u32[]{:S(2)}) collective-permute-start(f32[516,1,128]{2,1,0:T(1,128)} %get-tuple-element.71), channel_id=1, source_target_pairs={{0,2},{1,3},{2,0},{3,1},{4,6},{5,7},{6,4},{7,5},{8,10},{9,11},{10,... | collective-permute-start | bytes 792584 | tf_op jit(solution)/shard_map/ppermute | solution.py:350
  71.5 27.9 %collective-permute-start.18 = (f32[516,1,128]{2,1,0:T(1,128)}, f32[516,1,128]{2,1,0:T(1,128)S(1)}, u32[]{:S(2)}, u32[]{:S(2)}) collective-permute-start(f32[516,1,128]{2,1,0:T(1,128)} %get-tuple-element.72), channel_id=1, source_target_pairs={{0,24},{1,25},{2,26},{3,27},{4,28},{5,29},{6,30},{7,31},{8,16},{9,... | collective-permute-start | bytes 792584 | tf_op jit(solution)/shard_map/ppermute | solution.py:350
  72.4 14.9 %collective-permute-start.13 = (f32[258,1,128]{2,1,0:T(1,128)}, f32[258,1,128]{2,1,0:T(1,128)S(1)}, u32[]{:S(2)}, u32[]{:S(2)}) collective-permute-start(f32[258,1,128]{2,1,0:T(1,128)} %get-tuple-element.63), channel_id=1, source_target_pairs={{0,13},{1,12},{2,15},{3,14},{4,9},{5,8},{6,11},{7,10},{8,5},{9,4},... | collective-permute-start | bytes 396296 | tf_op jit(solution)/shard_map/ppermute | solution.py:350
  74.6 17.1 %collective-permute-start.14 = (f32[258,1,128]{2,1,0:T(1,128)}, f32[258,1,128]{2,1,0:T(1,128)S(1)}, u32[]{:S(2)}, u32[]{:S(2)}) collective-permute-start(f32[258,1,128]{2,1,0:T(1,128)} %get-tuple-element.64), channel_id=1, source_target_pairs={{0,14},{1,15},{2,12},{3,13},{4,10},{5,11},{6,8},{7,9},{8,6},{9,7},... | collective-permute-start | bytes 396296 | tf_op jit(solution)/shard_map/ppermute | solution.py:350
  75.7 18.9 %collective-permute-start.15 = (f32[258,1,128]{2,1,0:T(1,128)}, f32[258,1,128]{2,1,0:T(1,128)S(1)}, u32[]{:S(2)}, u32[]{:S(2)}) collective-permute-start(f32[258,1,128]{2,1,0:T(1,128)} %get-tuple-element.65), channel_id=1, source_target_pairs={{0,15},{1,14},{2,13},{3,12},{4,11},{5,10},{6,9},{7,8},{8,7},{9,6},... | collective-permute-start | bytes 396296 | tf_op jit(solution)/shard_map/ppermute | solution.py:350
  87.3 12.9 %collective-permute-start.19 = (f32[516,1,128]{2,1,0:T(1,128)}, f32[516,1,128]{2,1,0:T(1,128)S(1)}, u32[]{:S(2)}, u32[]{:S(2)}) collective-permute-start(f32[516,1,128]{2,1,0:T(1,128)} %get-tuple-element.73), channel_id=1, source_target_pairs={{0,26},{1,27},{2,24},{3,25},{4,30},{5,31},{6,28},{7,29},{8,18},{9,... | collective-permute-start | bytes 792584 | tf_op jit(solution)/shard_map/ppermute | solution.py:350
  91.6 31.8 %collective-permute-start.20 = (f32[516,1,128]{2,1,0:T(1,128)}, f32[516,1,128]{2,1,0:T(1,128)S(1)}, u32[]{:S(2)}, u32[]{:S(2)}) collective-permute-start(f32[516,1,128]{2,1,0:T(1,128)} %get-tuple-element.78), channel_id=1, source_target_pairs={{0,20},{1,21},{2,22},{3,23},{4,16},{5,17},{6,18},{7,19},{8,28},{9,... | collective-permute-start | bytes 792584 | tf_op jit(solution)/shard_map/ppermute | solution.py:350
  94.6 36.0 %collective-permute-start.21 = (f32[516,1,128]{2,1,0:T(1,128)}, f32[516,1,128]{2,1,0:T(1,128)S(1)}, u32[]{:S(2)}, u32[]{:S(2)}) collective-permute-start(f32[516,1,128]{2,1,0:T(1,128)} %get-tuple-element.79), channel_id=1, source_target_pairs={{0,22},{1,23},{2,20},{3,21},{4,18},{5,19},{6,16},{7,17},{8,30},{9,... | collective-permute-start | bytes 792584 | tf_op jit(solution)/shard_map/ppermute | solution.py:350
  98.3 51.5 %collective-permute-start.22 = (f32[516,1,128]{2,1,0:T(1,128)}, f32[516,1,128]{2,1,0:T(1,128)S(1)}, u32[]{:S(2)}, u32[]{:S(2)}) collective-permute-start(f32[516,1,128]{2,1,0:T(1,128)} %get-tuple-element.84), channel_id=1, source_target_pairs={{0,28},{1,29},{2,30},{3,31},{4,24},{5,25},{6,26},{7,27},{8,20},{9,... | collective-permute-start | bytes 792584 | tf_op jit(solution)/shard_map/ppermute | solution.py:350
  99.4 52.0 %collective-permute-start.23 = (f32[516,1,128]{2,1,0:T(1,128)}, f32[516,1,128]{2,1,0:T(1,128)S(1)}, u32[]{:S(2)}, u32[]{:S(2)}) collective-permute-start(f32[516,1,128]{2,1,0:T(1,128)} %get-tuple-element.89), channel_id=1, source_target_pairs={{0,30},{1,31},{2,28},{3,29},{4,26},{5,27},{6,24},{7,25},{8,22},{9,... | collective-permute-start | bytes 792584 | tf_op jit(solution)/shard_map/ppermute | solution.py:350
  100.2 51.1 %collective-permute-start.34 = (f32[64,128]{1,0:T(8,128)S(1)}, f32[64,128]{1,0:T(8,128)S(1)}, u32[]{:S(2)}, u32[]{:S(2)}) collective-permute-start(f32[64,128]{1,0:T(8,128)S(1)} %shard_map.74.refs_6_), channel_id=1, source_target_pairs={{0,24},{8,16},{16,8},{24,0},{1,25},{9,17},{17,9},{25,1},{2,26},{10... | collective-permute-start | bytes 98312 | tf_op jit(solution)/shard_map/ppermute | solution.py:350
  123.4 27.9 %collective-permute-start.33 = (f32[64,128]{1,0:T(8,128)S(1)}, f32[64,128]{1,0:T(8,128)S(1)}, u32[]{:S(2)}, u32[]{:S(2)}) collective-permute-start(f32[64,128]{1,0:T(8,128)S(1)} %shard_map.74.refs_6_), channel_id=1, source_target_pairs={{0,16},{8,24},{16,0},{24,8},{1,17},{9,25},{17,1},{25,9},{2,18},{10... | collective-permute-start | bytes 98312 | tf_op jit(solution)/shard_map/ppermute | solution.py:350
  130.6 20.8 %collective-permute-start.32 = (f32[64,128]{1,0:T(8,128)S(1)}, f32[64,128]{1,0:T(8,128)S(1)}, u32[]{:S(2)}, u32[]{:S(2)}) collective-permute-start(f32[64,128]{1,0:T(8,128)S(1)} %shard_map.74.refs_6_), channel_id=1, source_target_pairs={{0,8},{8,0},{16,24},{24,16},{1,9},{9,1},{17,25},{25,17},{2,10},{10... | collective-permute-start | bytes 98312 | tf_op jit(solution)/shard_map/ppermute | solution.py:350
  133.0 1.0 copy-start.1
  149.8 1.6 %copy-start.2 = (s32[256]{0:T(256)S(1)}, s32[256]{0:T(256)}, u32[]{:S(2)}) copy-start(s32[256]{0:T(256)} %refs_5_.1) | copy-start | bytes 3076
